TPU v7x, 32 devices: a whole 2x2x4 slice. The times are simulated.
32 devices in a mesh: seq: 8 (over z, y), batch: 4 (over x, core).
Axes of the slice: x: 2, y: 2, z: 4, core: 2. Of those that a mesh axis runs over, the one named last changes fastest.
Arguments:
- conv_input: bfloat16 [4096, 8192], P(('batch', 'seq')), parts along dimension 0, may hold values from -6 to 6
- gate_input: bfloat16 [4096, 8192], P(('batch', 'seq')), parts along dimension 0, may hold values from -6 to 6
- conv_weight: bfloat16 [4, 8192], P(None, 'seq'), may hold values from -3 to 3
- conv_bias: bfloat16 [8192], P('seq'), may hold values from -3 to 3
- x_weight: bfloat16 [8192, 288], P('seq'), may hold values from -0.0625 to 0.0625
- dt_gain: float32 [256], replicated, may hold values from 0.5 to 1.5
- dt_weight: bfloat16 [256, 8192], P(None, 'seq'), may hold values from -0.375 to 0.375
- dt_bias: float32 [8192], P('seq'), may hold values from -6.9 to -2.3
- a_log: float32 [16, 8192], P(None, 'seq'), may hold values from 0 to 2.77
- skip: float32 [8192], P('seq'), may hold values from 0.5 to 1.5
Outputs:
- mixed: bfloat16 [4096, 8192], P(('batch', 'seq')), parts along dimension 0
There are 4 independent parts, one for each index of `batch`. A program takes and returns all parts, laid end to end along the dimension named above; an argument that names none is the same for every part. Nothing has to cross between parts.
All inputs are finite; a program needn't handle non-finite values.
Results may differ from a plain program's by a relative error of at most 0.0085.
Values may be sent and summed in bfloat16 or wider, within the bound.
A program may use at most 128 MiB of HBM per device.

v0:
```python
import jax
import jax.numpy as jnp
from jax import lax
from jax.sharding import PartitionSpec as P


def causal_conv(prefix, inputs, weight, bias):
    rows = inputs.shape[0]
    width = weight.shape[0]
    padded = jnp.concatenate([prefix, inputs.astype(jnp.float32)], 0)
    total = bias.astype(jnp.float32)[None, :]
    for tap in range(width):
        total = total + weight[tap].astype(jnp.float32)[None, :] * padded[tap : tap + rows]
    return jax.nn.silu(total).astype(jnp.bfloat16)


def link_blocks(earlier, later):
    return (earlier[0] * later[0], later[0] * earlier[1] + later[1])


def selective_scan(step, xfloat, bmat, cmat, rate):
    span = 16
    length, chans = step.shape
    states = rate.shape[0]
    blocks = length // span
    step_rows = step.reshape(blocks, span * chans)
    drive_rows = (step * xfloat).reshape(blocks, span * chans)
    b_rows = bmat.reshape(blocks, span * states)
    c_rows = cmat.reshape(blocks, span * states)
    state = jnp.zeros((blocks, states, chans), jnp.float32)
    running = jnp.zeros((blocks, chans), jnp.float32)
    local_parts = []
    elapsed = []
    for place in range(span):
        step_now = step_rows[:, place * chans : (place + 1) * chans]
        drive_now = drive_rows[:, place * chans : (place + 1) * chans]
        b_now = b_rows[:, place * states : (place + 1) * states]
        c_now = c_rows[:, place * states : (place + 1) * states]
        state = (
            jnp.exp(step_now[:, None, :] * rate[None]) * state
            + b_now[:, :, None] * drive_now[:, None, :]
        )
        local_parts.append(jnp.sum(c_now[:, :, None] * state, axis=1))
        running = running + step_now
        elapsed.append(running)
    totals = jnp.exp(running[:, None, :] * rate[None])
    _, through = lax.associative_scan(link_blocks, (totals, state), axis=0)
    starts = jnp.concatenate([jnp.zeros((1, states, chans), jnp.float32), through[: blocks - 1]], 0)
    pieces = []
    for place in range(span):
        c_now = c_rows[:, place * states : (place + 1) * states]
        carried = jnp.sum(
            c_now[:, :, None] * jnp.exp(elapsed[place][:, None, :] * rate[None]) * starts, axis=1
        )
        pieces.append(local_parts[place] + carried)
    return jnp.concatenate(pieces, 1).reshape(length, chans)


def local(
    conv_input,
    gate_input,
    conv_weight,
    conv_bias,
    x_weight,
    dt_gain,
    dt_weight,
    dt_bias,
    a_log,
    skip,
):
    width = conv_weight.shape[0]
    rank = dt_weight.shape[0]
    states = a_log.shape[0]
    arrived = lax.all_to_all(conv_input, "seq", split_axis=1, concat_axis=0, tiled=True)
    zero_prefix = jnp.zeros((width - 1, arrived.shape[1]), jnp.float32)
    conv_out = causal_conv(zero_prefix, arrived, conv_weight, conv_bias)
    partial_value = jnp.dot(conv_out, x_weight, preferred_element_type=jnp.float32)
    proj = lax.psum(partial_value, "seq")
    dt_low = proj[:, :rank]
    bmat = proj[:, rank : rank + states]
    cmat = proj[:, rank + states :]
    normed = (
        dt_low
        * lax.rsqrt(jnp.mean(dt_low * dt_low, axis=1, keepdims=True) + 1e-06)
        * dt_gain[None, :]
    ).astype(jnp.bfloat16)
    step = jax.nn.softplus(
        jnp.dot(normed, dt_weight, preferred_element_type=jnp.float32) + dt_bias[None, :]
    )
    rate = -jnp.exp(a_log)
    xfloat = conv_out.astype(jnp.float32)
    scanned = selective_scan(step, xfloat, bmat, cmat, rate)
    y_out = (scanned + skip[None, :] * xfloat).astype(jnp.bfloat16)
    returned = lax.all_to_all(y_out, "seq", split_axis=0, concat_axis=1, tiled=True)
    return (returned.astype(jnp.float32) * jax.nn.silu(gate_input.astype(jnp.float32))).astype(
        jnp.bfloat16
    )


def solution(mesh):
    return jax.shard_map(
        local,
        mesh=mesh,
        in_specs=(
            P(("batch", "seq"), None),
            P(("batch", "seq"), None),
            P(None, "seq"),
            P("seq"),
            P("seq", None),
            P(),
            P(None, "seq"),
            P("seq"),
            P(None, "seq"),
            P("seq"),
        ),
        out_specs=P(("batch", "seq"), None),
        check_vma=False,
    )
```

profile of v0, /device:TPU:0, one launch (start us, length us, event | category | flops | bytes accessed | tf_op | source)
XLA Modules:
  0.0 461.8 jit_solution(15684360439202959962)
XLA Ops:
  9.8 7.3 %all-to-all-start = ((bf16[128,8,1024]{2,0,1:T(8,128)(2,1)}), bf16[128,8,1024]{2,0,1:T(8,128)(2,1)S(1)}, u32[]{:S(2)}, u32[]{:S(2)}) async-start(bf16[128,8,1024]{2,0,1:T(8,128)(2,1)} %bitcast.22), calls=%async_computation | async-start | bytes 4194304 | tf_op jit(solution)/shard_map/all_to_all | solution.py:74
  17.2 48.1 %all-to-all-done = bf16[128,8,1024]{2,0,1:T(8,128)(2,1)S(1)} async-done(((bf16[128,8,1024]{2,0,1:T(8,128)(2,1)}), bf16[128,8,1024]{2,0,1:T(8,128)(2,1)S(1)}, u32[]{:S(2)}, u32[]{:S(2)}) %all-to-all-start) | async-done | bytes 2097184 | tf_op jit(solution)/shard_map/all_to_all | solution.py:74
  72.4 79.5 %all-reduce.16.cloned.1.call-done = f32[1024,288]{0,1:T(8,128)} async-done(((f32[1024,288]{0,1:T(8,128)}), f32[1024,288]{0,1:T(8,128)}) %all-reduce.16.cloned.1.call-update) | async-done | bytes 1179664 | tf_op jit(solution)/shard_map/psum | solution.py:78
  153.3 7.3 %convert_multiply_fusion.2 = (f32[1024,1024]{1,0:T(8,128)}, f32[1024,1024]{1,0:T(8,128)}) fusion(bf16[1024,1024]{1,0:T(8,128)(2,1)S(1)} %multiply_convert_fusion, f32[1024]{0:T(1024)S(1)} %copy-done.125, bf16[256,1024]{1,0:T(8,128)(2,1)S(1)} %copy-done.124, f32[1024,288]{0,1:T(8,128)} %all-reduce.16.cloned.1.call-done, f32[256]{0:T(256)S(1)} %copy-done.126, ...), kind=kOutput, calls=%fused_computation.4 | convolution fusion | flops 547094528 | bytes 12067840 | tf_op jit(solution)/shard_map/dot_general | solution.py:88
  160.6 5.0 %reshape.118 = f32[64,16384]{1,0:T(8,128)} reshape(f32[1024,1024]{1,0:T(8,128)} %get-tuple-element.143) | data formatting | bytes 8388608 | tf_op jit(solution)/shard_map/reshape | solution.py:26
  175.3 5.1 %reshape.120 = f32[64,16384]{1,0:T(8,128)} reshape(f32[1024,1024]{1,0:T(8,128)} %get-tuple-element.142) | data formatting | bytes 8388608 | tf_op jit(solution)/shard_map/reshape | solution.py:27
  184.2 23.0 %multiply_reduce_fusion.1 = (f32[64,1024]{1,0:T(8,128)}, f32[64,16,1024]{2,1,0:T(8,128)S(1)}, f32[64,16,1024]{2,1,0:T(8,128)}, f32[64,16,1024]{2,1,0:T(8,128)}) fusion(f32[64,16]{1,0:T(8,128)} %get-tuple-element.107, f32[64,1024]{1,0:T(8,128)} %get-tuple-element.75, f32[64,16]{1,0:T(8,128)} %get-tuple-element.123, f32[64,1024]{1,0:T(8,128)S(1)} %get-tuple-element.76, ...), kind=kLoop, calls=%fused_computation.13 | loop fusion | flops 69140480 | bytes 21368832 | tf_op jit(solution)/shard_map/reduce_sum | solution.py:43
  207.9 7.9 %multiply_reduce_fusion.3 = (f32[64,1024]{1,0:T(8,128)}, f32[64,1024]{1,0:T(8,128)}, f32[64,1024]{1,0:T(8,128)}, f32[64,16,1024]{2,1,0:T(8,128)S(1)}) fusion(f32[64,16]{1,0:T(8,128)S(1)} %get-tuple-element.108, f32[64,1024]{1,0:T(8,128)S(1)} %get-tuple-element.76, f32[64,16]{1,0:T(8,128)} %get-tuple-element.124, f32[64,1024]{1,0:T(8,128)S(1)} %get-tuple-element.77, ...), kind=kLoop, calls=%fused_computation.15 | loop fusion | flops 15532032 | bytes 10571776 | tf_op jit(solution)/shard_map/reduce_sum | solution.py:43
  236.3 5.7 %pad.46 = f32[16,16,1024]{2,1,0:T(8,128)} pad(f32[8,16,1024]{2,1,0:T(8,128)} %add.325, f32[]{:T(128)} %constant.4.clone.1), padding=1_0_1x0_0_0x0_0_0 | pad | bytes 1572868 | tf_op jit(solution)/shard_map/pad | solution.py:47
  246.6 7.0 %pad.47 = f32[32,16,1024]{2,1,0:T(8,128)S(1)} pad(f32[16,16,1024]{2,1,0:T(8,128)} %pad_maximum_fusion.1, f32[]{:T(128)} %constant.4.clone.1), padding=0_1_1x0_0_0x0_0_0 | pad | bytes 3145732 | tf_op jit(solution)/shard_map/pad | solution.py:47
  253.6 10.2 %pad.48 = f32[32,16,1024]{2,1,0:T(8,128)} pad(f32[16,16,1024]{2,1,0:T(8,128)} %add.327, f32[]{:T(128)} %constant.4.clone.1), padding=1_0_1x0_0_0x0_0_0 | pad | bytes 3145732 | tf_op jit(solution)/shard_map/pad | solution.py:47
  270.6 9.1 %multiply_reduce_fusion.17 = f32[64,1024]{1,0:T(8,128)} fusion(f32[64,16]{1,0:T(8,128)S(1)} %copy-done.96, f32[64,1024]{1,0:T(8,128)S(1)} %copy-done.68, f32[64,16]{1,0:T(8,128)S(1)} %copy-done.120, f32[64,1024]{1,0:T(8,128)S(1)} %copy-done.79, f32[16,1024]{1,0:T(8,128)S(1)} %exponential_negate_fusion, f32[64,1024]{1,0:T(8,128)S(1)} %copy-done.67, ...), kind=kLoop, calls=%fused_computation.29 | loop fusion | flops 35586048 | bytes 4558848 | tf_op jit(solution)/shard_map/reduce_sum | solution.py:43
  279.8 8.2 %multiply_reduce_fusion.19 = f32[64,1024]{1,0:T(8,128)} fusion(f32[64,16]{1,0:T(8,128)S(1)} %copy-done.98, f32[64,1024]{1,0:T(8,128)S(1)} %copy-done.67, f32[64,16]{1,0:T(8,128)S(1)} %copy-done.119, f32[64,1024]{1,0:T(8,128)S(1)} %copy-done.65, f32[64,16]{1,0:T(8,128)S(1)} %copy-done.118, f32[64,1024]{1,0:T(8,128)S(1)} %copy-done.77, ...), kind=kLoop, calls=%fused_computation.31 | loop fusion | flops 31391744 | bytes 4030464 | tf_op jit(solution)/shard_map/reduce_sum | solution.py:43
  287.9 7.0 %multiply_reduce_fusion.21 = f32[64,1024]{1,0:T(8,128)} fusion(f32[64,16]{1,0:T(8,128)S(1)} %copy-done.101, f32[64,1024]{1,0:T(8,128)S(1)} %copy-done.65, f32[64,16]{1,0:T(8,128)S(1)} %copy-done.118, f32[64,1024]{1,0:T(8,128)S(1)} %copy-done.77, f32[16,1024]{1,0:T(8,128)S(1)} %exponential_negate_fusion, f32[64,1024]{1,0:T(8,128)S(1)} %copy-done.57, ...), kind=kLoop, calls=%fused_computation.33 | loop fusion | flops 27197440 | bytes 3502080 | tf_op jit(solution)/shard_map/reduce_sum | solution.py:43
  296.4 18.5 %pad.62 = f32[63,16,1024]{2,1,0:T(8,128)} pad(f32[32,16,1024]{2,1,0:T(8,128)} %pad_maximum_fusion, f32[]{:T(128)} %constant.4.clone.1), padding=0_0_1x0_0_0x0_0_0 | pad | bytes 6225924 | tf_op jit(solution)/shard_map/slice | solution.py:48
  314.9 12.1 %pad.86 = f32[64,16,1024]{2,1,0:T(8,128)} pad(f32[32,16,1024]{2,1,0:T(8,128)S(1)} %copy-done.10, f32[]{:T(128)} %constant.4.clone.1), padding=1_0_1x0_0_0x0_0_0 | pad | bytes 6291460
  331.7 9.3 %multiply_reduce_fusion.29 = (f32[64,1024]{1,0:T(8,128)S(1)}, f32[64,1024]{1,0:T(8,128)S(1)}, f32[64,1024]{1,0:T(8,128)S(1)}, f32[64,1024]{1,0:T(8,128)S(1)}, f32[64,1024]{1,0:T(8,128)S(1)}, /*index=5*/f32[64,1024]{1,0:T(8,128)S(1)}) fusion(f32[64,16]{1,0:T(8,128)S(1)} %copy-done.106, f32[64,1024]{1,0:T(8,128)S(1)} %copy-done.62, ...), kind=kLoop, calls=%fused_computation.41 | loop fusion | flops 27918336 | bytes 7630848 | tf_op jit(solution)/shard_map/reduce_sum | solution.py:43
  341.9 7.3 %multiply_reduce_fusion.23 = (f32[64,1024]{1,0:T(8,128)S(1)}, f32[64,1024]{1,0:T(8,128)S(1)}, f32[64,1024]{1,0:T(8,128)S(1)}) fusion(f32[64,16]{1,0:T(8,128)S(1)} %copy-done.103, f32[64,1024]{1,0:T(8,128)S(1)} %copy-done.58, f32[64,16]{1,0:T(8,128)S(1)} %copy-done.110, f32[64,1024]{1,0:T(8,128)S(1)} %copy-done.60, f32[64,16]{1,0:T(8,128)S(1)} %copy-done.112, ...), kind=kLoop, calls=%fused_computation.35 | loop fusion | flops 27066368 | bytes 3506176 | tf_op jit(solution)/shard_map/reduce_sum | solution.py:43
  349.4 9.2 %multiply_reduce_fusion = (f32[64,1024]{1,0:T(8,128)S(1)}, f32[64,1024]{1,0:T(8,128)S(1)}, f32[64,1024]{1,0:T(8,128)S(1)}, f32[64,1024]{1,0:T(8,128)S(1)}, f32[64,1024]{1,0:T(8,128)S(1)}, /*index=5*/f32[64,1024]{1,0:T(8,128)S(1)}) fusion(f32[64,16]{1,0:T(8,128)S(1)} %copy-done.100, f32[16,1024]{1,0:T(8,128)S(1)} %exponential_negate_fusion, ...), kind=kLoop, calls=%fused_computation.12 | loop fusion | flops 24772608 | bytes 7364608 | tf_op jit(solution)/shard_map/reduce_sum | solution.py:52
  362.4 5.9 %multiply_reduce_fusion.9 = (f32[64,1024]{1,0:T(8,128)S(1)}, f32[64,1024]{1,0:T(8,128)S(1)}, f32[64,1024]{1,0:T(8,128)S(1)}, f32[64,1024]{1,0:T(8,128)S(1)}) fusion(f32[64,16]{1,0:T(8,128)S(1)} %copy-done.90, f32[64,1024]{1,0:T(8,128)S(1)} %copy-done.16, f32[64,16]{1,0:T(8,128)S(1)} %copy-done.86, f32[64,1024]{1,0:T(8,128)S(1)} %copy-done.26, ...), kind=kLoop, calls=%fused_computation.21 | loop fusion | flops 20709376 | bytes 6909952 | tf_op jit(solution)/shard_map/reduce_sum | solution.py:43
  368.4 9.0 %multiply_reduce_fusion.2 = (f32[64,1024]{1,0:T(8,128)S(1)}, f32[64,1024]{1,0:T(8,128)S(1)}, f32[64,1024]{1,0:T(8,128)S(1)}, f32[64,1024]{1,0:T(8,128)S(1)}, f32[64,1024]{1,0:T(8,128)S(1)}, /*index=5*/f32[64,1024]{1,0:T(8,128)S(1)}) fusion(f32[64,1024]{1,0:T(8,128)S(1)} %copy-done.33, f32[64,16]{1,0:T(8,128)S(1)} %copy-done.82, ...), kind=kLoop, calls=%fused_computation.14 | loop fusion | flops 24772608 | bytes 7364608 | tf_op jit(solution)/shard_map/reduce_sum | solution.py:52
  384.9 5.0 %reshape.121 = f32[1024,1024]{1,0:T(8,128)} reshape(f32[64,16384]{1,0:T(8,128)} %add_dynamic-update-slice_fusion) | data formatting | bytes 8388608 | tf_op jit(solution)/shard_map/reshape | solution.py:56
  389.9 9.1 %fusion.1 = bf16[1024,1024]{1,0:T(8,128)(2,1)S(1)} fusion(f32[1024,1024]{1,0:T(8,128)} %reshape.121, f32[1024]{0:T(1024)S(1)} %copy-done.122, f32[1024,1024]{1,0:T(8,128)} %bitcast.20, f32[1024]{0:T(1024)S(1)} %bitcast.30, f32[1024]{0:T(1024)S(1)} %bitcast.32, f32[1024]{0:T(1024)S(1)} %bitcast.28, f32[1024]{0:T(1024)S(1)} %bitcast.26, ...), kind=kLoop, calls=%fused_computation.6 | loop fusion | flops 17825792 | bytes 10510336 | tf_op jit(solution)/shard_map/convert_element_type | solution.py:93
  399.0 51.4 %all_to_all.26 = bf16[8,128,1024]{2,1,0:T(8,128)(2,1)S(1)} all-to-all(bf16[8,128,1024]{2,1,0:T(8,128)(2,1)S(1)} %bitcast.23), channel_id=1, replica_groups=mesh['seq'=8,'batch'=4] {'seq'}, dimensions={0} | all-to-all | bytes 4194304 | tf_op jit(solution)/shard_map/all_to_all | solution.py:94
  (325 shorter events, 79.7 us)
Async XLA Ops:
  6.5 63.9 %copy-start = (bf16[1024,288]{0,1:T(8,128)(2,1)S(1)}, bf16[1024,288]{0,1:T(8,128)(2,1)}, u32[]{:S(2)}) copy-start(bf16[1024,288]{0,1:T(8,128)(2,1)} %param.14) | copy-start | bytes 1769476
  9.8 55.5 %all-to-all-start = ((bf16[128,8,1024]{2,0,1:T(8,128)(2,1)}), bf16[128,8,1024]{2,0,1:T(8,128)(2,1)S(1)}, u32[]{:S(2)}, u32[]{:S(2)}) async-start(bf16[128,8,1024]{2,0,1:T(8,128)(2,1)} %bitcast.22), calls=%async_computation | async-start | bytes 4194304 | tf_op jit(solution)/shard_map/all_to_all | solution.py:74
  17.1 134.9 %all-reduce.16.cloned.1.call-start = ((), (), s32[]{:S(2)}) async-start(), calls=%async_computation.2 | async-start | bytes 2359296 | tf_op jit(solution)/shard_map/psum | solution.py:78
  17.2 48.6 %copy-start.94 = (f32[1,1024]{1,0:T(1,128)}, f32[1,1024]{1,0:T(1,128)S(1)}, u32[]{:S(2)}) copy-start(f32[1,1024]{1,0:T(1,128)S(1)} %get-tuple-element.141) | copy-start | bytes 12292
  70.5 82.8 %copy-start.124 = (bf16[256,1024]{1,0:T(8,128)(2,1)S(1)}, bf16[256,1024]{1,0:T(8,128)(2,1)}, u32[]{:S(2)}) copy-start(bf16[256,1024]{1,0:T(8,128)(2,1)} %param.16) | copy-start | bytes 1572868
  70.5 82.8 %copy-start.125 = (f32[1024]{0:T(1024)S(1)}, f32[1024]{0:T(1024)}, u32[]{:S(2)}) copy-start(f32[1024]{0:T(1024)} %param.17) | copy-start | bytes 12292
  70.5 82.8 %copy-start.126 = (f32[256]{0:T(256)S(1)}, f32[256]{0:T(256)}, u32[]{:S(2)}) copy-start(f32[256]{0:T(256)} %param.15) | copy-start | bytes 3076
  169.3 14.9 %copy-start.21 = (f32[64,1024]{1,0:T(8,128)}, f32[64,1024]{1,0:T(8,128)S(1)}, u32[]{:S(2)}) copy-start(f32[64,1024]{1,0:T(8,128)S(1)} %get-tuple-element.66) | copy-start | bytes 786436
  169.3 14.9 %copy-start.23 = (f32[64,1024]{1,0:T(8,128)}, f32[64,1024]{1,0:T(8,128)S(1)}, u32[]{:S(2)}) copy-start(f32[64,1024]{1,0:T(8,128)S(1)} %get-tuple-element.67) | copy-start | bytes 786436
  169.3 14.9 %copy-start.25 = (f32[64,1024]{1,0:T(8,128)}, f32[64,1024]{1,0:T(8,128)S(1)}, u32[]{:S(2)}) copy-start(f32[64,1024]{1,0:T(8,128)S(1)} %get-tuple-element.68) | copy-start | bytes 786436
  171.4 36.5 %copy-start.28 = (f32[64,1024]{1,0:T(8,128)}, f32[64,1024]{1,0:T(8,128)S(1)}, u32[]{:S(2)}) copy-start(f32[64,1024]{1,0:T(8,128)S(1)} %get-tuple-element.41) | copy-start | bytes 786436
  175.3 32.6 %copy-start.81 = (f32[64,16]{1,0:T(8,128)}, f32[64,16]{1,0:T(8,128)S(1)}, u32[]{:S(2)}) copy-start(f32[64,16]{1,0:T(8,128)S(1)} %get-tuple-element.108) | copy-start | bytes 12292
  184.1 23.1 %copy-start.15 = (f32[64,1024]{1,0:T(8,128)}, f32[64,1024]{1,0:T(8,128)S(1)}, u32[]{:S(2)}) copy-start(f32[64,1024]{1,0:T(8,128)S(1)} %get-tuple-element.79) | copy-start | bytes 786436
  184.1 23.1 %copy-start.17 = (f32[64,1024]{1,0:T(8,128)}, f32[64,1024]{1,0:T(8,128)S(1)}, u32[]{:S(2)}) copy-start(f32[64,1024]{1,0:T(8,128)S(1)} %get-tuple-element.80) | copy-start | bytes 786436
  184.1 23.1 %copy-start.19 = (f32[64,1024]{1,0:T(8,128)}, f32[64,1024]{1,0:T(8,128)S(1)}, u32[]{:S(2)}) copy-start(f32[64,1024]{1,0:T(8,128)S(1)} %get-tuple-element.81) | copy-start | bytes 786436
  184.1 23.1 %copy-start.54 = (f32[64,1024]{1,0:T(8,128)}, f32[64,1024]{1,0:T(8,128)S(1)}, u32[]{:S(2)}) copy-start(f32[64,1024]{1,0:T(8,128)S(1)} %get-tuple-element.74) | copy-start | bytes 786436
  294.9 19.9 %copy-start.10 = (f32[32,16,1024]{2,1,0:T(8,128)S(1)}, f32[32,16,1024]{2,1,0:T(8,128)}, u32[]{:S(2)}) copy-start(f32[32,16,1024]{2,1,0:T(8,128)} %add.329) | copy-start | bytes 6291460
  349.3 13.1 %copy-start.13 = (f32[64,16,1024]{2,1,0:T(8,128)S(1)}, f32[64,16,1024]{2,1,0:T(8,128)}, u32[]{:S(2)}) copy-start(f32[64,16,1024]{2,1,0:T(8,128)} %get-tuple-element.40) | copy-start | bytes 12582916
  349.3 13.1 %copy-start.16 = (f32[64,1024]{1,0:T(8,128)S(1)}, f32[64,1024]{1,0:T(8,128)}, u32[]{:S(2)}) copy-start(f32[64,1024]{1,0:T(8,128)} %copy-done.15) | copy-start | bytes 786436
  349.3 13.1 %copy-start.18 = (f32[64,1024]{1,0:T(8,128)S(1)}, f32[64,1024]{1,0:T(8,128)}, u32[]{:S(2)}) copy-start(f32[64,1024]{1,0:T(8,128)} %copy-done.17) | copy-start | bytes 786436
  349.3 13.1 %copy-start.20 = (f32[64,1024]{1,0:T(8,128)S(1)}, f32[64,1024]{1,0:T(8,128)}, u32[]{:S(2)}) copy-start(f32[64,1024]{1,0:T(8,128)} %copy-done.19) | copy-start | bytes 786436
  349.3 13.1 %copy-start.22 = (f32[64,1024]{1,0:T(8,128)S(1)}, f32[64,1024]{1,0:T(8,128)}, u32[]{:S(2)}) copy-start(f32[64,1024]{1,0:T(8,128)} %copy-done.21) | copy-start | bytes 786436
  349.3 13.1 %copy-start.24 = (f32[64,1024]{1,0:T(8,128)S(1)}, f32[64,1024]{1,0:T(8,128)}, u32[]{:S(2)}) copy-start(f32[64,1024]{1,0:T(8,128)} %copy-done.23) | copy-start | bytes 786436
  349.3 13.1 %copy-start.26 = (f32[64,1024]{1,0:T(8,128)S(1)}, f32[64,1024]{1,0:T(8,128)}, u32[]{:S(2)}) copy-start(f32[64,1024]{1,0:T(8,128)} %copy-done.25) | copy-start | bytes 786436
  (105 other events, 630.9 us)
Sparse Core Ops, SparseCore 0:
  72.5 79.4 all-reduce.15
where the time goes:
time: 465 us; the launch traced here: 462 us
  other arithmetic  151 us (32%)
  waiting for transfers between devices  128 us (28%)
  local copies, waits for them, and re-layouts  100 us (22%)
  blocking collectives  51.4 us (11%)
  between operations  15 us (3%)
  matrix products  9.11 us (2%)
  starting transfers between devices  7.35 us (2%)
    psum x1, waiting for transfers between devices, local(): proj = lax.psum(partial_value, 'seq')  79.5 us
    reduce_sum x8, other arithmetic, selective_scan(): local_parts.append(jnp.sum(c_now[:, :, None] * state, axis=1))  77.7 us
    all_to_all x1, blocking collectives, local(): lax.all_to_all(y_out, 'seq', split_axis=0, concat_axis=1, tiled=True)  51.4 us
    all_to_all x1, waiting for transfers between devices, local(): lax.all_to_all(conv_input, 'seq', split_axis=1, concat_axis=0, tiled=True)  48.1 us
    pad x8, local copies, waits for them, and re-layouts, selective_scan(): _, through = lax.associative_scan(link_blocks, (totals, state), axis=0)  31.3 us
    slice x1, local copies, waits for them, and re-layouts, selective_scan(): through[:blocks - 1]  18.5 us
    unnamed x255, local copies, waits for them, and re-layouts  18.3 us
    reduce_sum x2, other arithmetic, selective_scan(): jnp.sum(c_now[:, :, None] * jnp.exp(elapsed[place][:, None, :] * rate[Non...  18.2 us
  transfers between devices with their start and end apart: 2, of which 2 were waited for; matrix products, arithmetic and copies ran while one was open for 0% of the time, Pallas kernels for 0%

commit v1 on v0

v1 whole, which is shorter than its diff:
```python
import functools

import jax
import jax.numpy as jnp
from jax import lax
from jax.experimental import pallas as pl
from jax.experimental.pallas import tpu as pltpu
from jax.sharding import PartitionSpec as P

LOG2E = 1.4426950408889634
HALO = 8


def conv_kernel(width, x_ref, halo_ref, w_ref, b_ref, xw_ref, xc_ref, part_ref, prev):
    rows, chans = x_ref.shape
    chunk = min(chans, 256)

    @pl.when(pl.program_id(1) == 0)
    def _():
        prev[...] = halo_ref[0]

    for start in range(0, chans, chunk):
        sl = slice(start, start + chunk)
        cur = x_ref[:, sl].astype(jnp.float32)
        ext = jnp.concatenate([prev[:, sl], cur], 0)
        total = b_ref[:, sl] + jnp.zeros((rows, chunk), jnp.float32)
        for tap in range(width):
            low = HALO - width + 1 + tap
            total = total + w_ref[tap : tap + 1, sl] * ext[low : low + rows]
        xc_ref[:, sl] = (total / (1.0 + jnp.exp(-total))).astype(jnp.bfloat16)
        prev[:, sl] = cur[rows - HALO :]
    part_ref[...] = jnp.dot(xc_ref[...], xw_ref[...], preferred_element_type=jnp.float32)


def conv_project(arrived, halo, weight, bias, x_weight, parts, block):
    total, chans = arrived.shape
    steps = total // parts // block
    cols = x_weight.shape[1]
    width = weight.shape[0]
    whole = lambda p, i: (0, 0)
    return pl.pallas_call(
        functools.partial(conv_kernel, width),
        grid=(parts, steps),
        in_specs=[
            pl.BlockSpec((block, chans), lambda p, i: (p * steps + i, 0)),
            pl.BlockSpec((1, HALO, chans), lambda p, i: (p, 0, 0)),
            pl.BlockSpec((width, chans), whole),
            pl.BlockSpec((1, chans), whole),
            pl.BlockSpec((chans, cols), whole),
        ],
        out_specs=[
            pl.BlockSpec((block, chans), lambda p, i: (p * steps + i, 0)),
            pl.BlockSpec((block, cols), lambda p, i: (p * steps + i, 0)),
        ],
        out_shape=[
            jax.ShapeDtypeStruct((total, chans), jnp.bfloat16),
            jax.ShapeDtypeStruct((total, cols), jnp.float32),
        ],
        scratch_shapes=[pltpu.VMEM((HALO, chans), jnp.float32)],
        name="conv_project",
    )(arrived, halo, weight.astype(jnp.float32), bias.astype(jnp.float32)[None, :], x_weight)


def scan_kernel(
    states, xc_ref, nm_ref, bc_ref, dtw_ref, dtb_ref, rate_ref, skip_ref, h0_ref, y_ref, st, dr, ys, hs
):
    rows, chans = xc_ref.shape
    group = chans // 128

    @pl.when(pl.program_id(1) == 0)
    def _():
        hs[...] = h0_ref[0]

    raw = jnp.dot(nm_ref[...], dtw_ref[...], preferred_element_type=jnp.float32) + dtb_ref[...]
    step = jnp.maximum(raw, 0.0) + jnp.log1p(jnp.exp(-jnp.abs(raw)))
    drive = step * xc_ref[...].astype(jnp.float32)
    for j in range(group):
        st[pl.ds(j, rows, stride=group), :] = step[:, j * 128 : (j + 1) * 128]
        dr[pl.ds(j, rows, stride=group), :] = drive[:, j * 128 : (j + 1) * 128]

    rates = [rate_ref[n * group : (n + 1) * group, :] for n in range(states)]

    def advance(t, hidden):
        at = pl.ds(pl.multiple_of(t * group, group), group)
        s = st[at, :]
        d = dr[at, :]
        base = t * (2 * states)
        after = []
        sums = [None, None]
        for n in range(states):
            h = jnp.exp2(s * rates[n]) * hidden[n] + bc_ref[0, 0, base + n] * d
            after.append(h)
            term = bc_ref[0, 0, base + states + n] * h
            sums[n % 2] = term if sums[n % 2] is None else sums[n % 2] + term
        ys[at, :] = sums[0] + sums[1]
        return tuple(after)

    hidden = tuple(hs[n * group : (n + 1) * group, :] for n in range(states))
    hidden = lax.fori_loop(0, rows, advance, hidden, unroll=4)
    for n in range(states):
        hs[n * group : (n + 1) * group, :] = hidden[n]
    for j in range(group):
        sl = slice(j * 128, (j + 1) * 128)
        y = ys[pl.ds(j, rows, stride=group), :] + skip_ref[:, sl] * xc_ref[:, sl].astype(jnp.float32)
        y_ref[:, sl] = y.astype(jnp.bfloat16)


def scan(xc, normed, bc, dt_weight, dt_bias, rate2, skip, start, parts, block):
    total, chans = xc.shape
    states2 = bc.shape[1]
    states = states2 // 2
    group = chans // 128
    steps = total // parts // block
    rank = normed.shape[1]
    whole = lambda p, i: (0, 0)
    tile = lambda p, i: (p * steps + i, 0)
    return pl.pallas_call(
        functools.partial(scan_kernel, states),
        grid=(parts, steps),
        in_specs=[
            pl.BlockSpec((block, chans), tile),
            pl.BlockSpec((block, rank), tile),
            pl.BlockSpec(
                (1, 1, block * states2), lambda p, i: (p * steps + i, 0, 0), memory_space=pltpu.SMEM
            ),
            pl.BlockSpec((rank, chans), whole),
            pl.BlockSpec((1, chans), whole),
            pl.BlockSpec((states * group, 128), whole),
            pl.BlockSpec((1, chans), whole),
            pl.BlockSpec((1, states * group, 128), lambda p, i: (p, 0, 0)),
        ],
        out_specs=pl.BlockSpec((block, chans), tile),
        out_shape=jax.ShapeDtypeStruct((total, chans), jnp.bfloat16),
        scratch_shapes=[
            pltpu.VMEM((block * group, 128), jnp.float32),
            pltpu.VMEM((block * group, 128), jnp.float32),
            pltpu.VMEM((block * group, 128), jnp.float32),
            pltpu.VMEM((states * group, 128), jnp.float32),
        ],
        name="selective_scan",
    )(
        xc,
        normed,
        bc.reshape(parts * steps, 1, block * states2),
        dt_weight,
        dt_bias[None, :],
        rate2.reshape(states * group, 128),
        skip[None, :],
        start,
    )


def local(
    conv_input,
    gate_input,
    conv_weight,
    conv_bias,
    x_weight,
    dt_gain,
    dt_weight,
    dt_bias,
    a_log,
    skip,
):
    rank, chans = dt_weight.shape
    states = a_log.shape[0]
    rows = conv_input.shape[0]
    arrived = lax.all_to_all(conv_input, "seq", split_axis=1, concat_axis=0, tiled=True)
    halo = jnp.zeros((1, HALO, chans), jnp.float32)
    conv_out, partial_value = conv_project(
        arrived, halo, conv_weight, conv_bias, x_weight, 1, rows
    )
    shares = lax.all_to_all(
        partial_value.reshape(-1, rows, partial_value.shape[1]), "seq", split_axis=0, concat_axis=0
    )
    proj = jnp.sum(shares, axis=0)
    dt_low = proj[:, :rank]
    bc = proj[:, rank:]
    normed = (
        dt_low
        * lax.rsqrt(jnp.mean(dt_low * dt_low, axis=1, keepdims=True) + 1e-06)
        * dt_gain[None, :]
    ).astype(jnp.bfloat16)
    high = lax.reduce_precision(bc, 8, 7)
    low = (bc - high).astype(jnp.bfloat16)
    packed = jnp.concatenate([normed, high.astype(jnp.bfloat16), low], 1)
    everyone = lax.all_gather(packed, "seq", axis=0, tiled=True)
    normed_all = everyone[:, :rank]
    bc_all = everyone[:, rank : rank + 2 * states].astype(jnp.float32) + everyone[
        :, rank + 2 * states :
    ].astype(jnp.float32)
    rate2 = -jnp.exp(a_log) * LOG2E
    start = jnp.zeros((1, states * chans // 128, 128), jnp.float32)
    y_out = scan(conv_out, normed_all, bc_all, dt_weight, dt_bias, rate2, skip, start, 1, rows)
    returned = lax.all_to_all(y_out, "seq", split_axis=0, concat_axis=1, tiled=True)
    return (returned.astype(jnp.float32) * jax.nn.silu(gate_input.astype(jnp.float32))).astype(
        jnp.bfloat16
    )


def solution(mesh):
    return jax.shard_map(
        local,
        mesh=mesh,
        in_specs=(
            P(("batch", "seq"), None),
            P(("batch", "seq"), None),
            P(None, "seq"),
            P("seq"),
            P("seq", None),
            P(),
            P(None, "seq"),
            P("seq"),
            P(None, "seq"),
            P("seq"),
        ),
        out_specs=P(("batch", "seq"), None),
        check_vma=False,
    )
```

time: 465 us -> 220 us (0.47)
  other arithmetic: 151 us -> 4.66 us
  local copies, waits for them, and re-layouts: 100 us -> 13.4 us
  waiting for transfers between devices: 128 us -> 74 us
  Pallas kernels: 0 us -> 37.9 us
  blocking collectives: 51.4 us -> 78.3 us
  between operations: 15 us -> 0.13 us
  matrix products: 9.11 us -> 0 us
    reduce_sum x10 -> x1, other arithmetic: 95.9 us -> 0.07 us  [local(): proj = jnp.sum(shares, axis=0)]
    psum x1 -> x0, waiting for transfers between devices: 79.5 us -> none  [local(): proj = lax.psum(partial_value, 'seq')]
    pallas_call x0 -> x2, Pallas kernels: none -> 37.9 us  [the longest x1 29.6 us: scan(): pl.pallas_call(functools.partial(scan_kernel, states), grid=(parts, steps...]
    all_gather x0 -> x1, blocking collectives: none -> 32.2 us  [local(): everyone = lax.all_gather(packed, 'seq', axis=0, tiled=True)]
    pad x8 -> x0, local copies, waits for them, and re-layouts: 31.3 us -> none  [selective_scan(): _, through = lax.associative_scan(link_blocks, (totals, state), axis=0)]
    slice x12 -> x3, local copies, waits for them, and re-layouts: 31.6 us -> 0.85 us  [the longest x1 0.83 us: local(): normed_all = everyone[:, :rank]]
    all_to_all x0 -> x1, waiting for transfers between devices: none -> 28.1 us  [local(): lax.all_to_all(partial_value.reshape(-1, rows, partial_value.shape[1]), '...]
    add x11 -> x1, other arithmetic: 21.1 us -> 0.14 us  [local(): everyone[:, rank:rank + 2 * states].astype(jnp.float32)]
  transfers between devices with their start and end apart: 2 -> 2, of which waited for: 2 -> 2; matrix products, arithmetic and copies ran while one was open for 0% -> 1% of each run, Pallas kernels for 0% -> 0%
where the time goes in v1:
time: 220 us
  blocking collectives  78.3 us (36%)
  waiting for transfers between devices  74 us (34%)
  Pallas kernels  37.9 us (17%)
  local copies, waits for them, and re-layouts  13.4 us (6%)
  starting transfers between devices  11.2 us (5%)
  other arithmetic  4.66 us (2%)
    all_to_all x1, blocking collectives, local(): lax.all_to_all(y_out, 'seq', split_axis=0, concat_axis=1, tiled=True)  46.1 us
    all_to_all x1, waiting for transfers between devices, local(): lax.all_to_all(conv_input, 'seq', split_axis=1, concat_axis=0, tiled=True)  45.9 us
    all_gather x1, blocking collectives, local(): everyone = lax.all_gather(packed, 'seq', axis=0, tiled=True)  32.2 us
    pallas_call x1, Pallas kernels, scan(): pl.pallas_call(functools.partial(scan_kernel, states), grid=(parts, steps...  29.6 us
    all_to_all x1, waiting for transfers between devices, local(): lax.all_to_all(partial_value.reshape(-1, rows, partial_value.shape[1]), '...  28.1 us
    pallas_call x1, Pallas kernels, conv_project(): pl.pallas_call(functools.partial(conv_kernel, width), grid=(parts, steps)...  8.37 us
    all_to_all x1, starting transfers between devices, local(): lax.all_to_all(conv_input, 'seq', split_axis=1, concat_axis=0, tiled=True)  7.44 us
  transfers between devices with their start and end apart: 2, of which 2 were waited for; matrix products, arithmetic and copies ran while one was open for 1% of the time, Pallas kernels for 0%

profile of v1, /device:TPU:0, one launch (start us, length us, event | category | flops | bytes accessed | tf_op | source)
XLA Modules:
  0.0 219.5 jit_solution(6001174949906446262)
XLA Ops:
  0.0 3.1 %copy.42 = bf16[16,8,8,1024]{3,2,0,1:T(8,128)(2,1)} copy(bf16[16,8,8,1024]{3,2,1,0:T(8,128)(2,1)} %bitcast.20) | data formatting | bytes 4194304 | tf_op jit(solution)/shard_map/all_to_all | solution.py:168
  3.2 7.4 %all-to-all-start = ((bf16[128,8,1024]{2,0,1:T(8,128)(2,1)}), bf16[128,8,1024]{2,0,1:T(8,128)(2,1)S(1)}, u32[]{:S(2)}, u32[]{:S(2)}) async-start(bf16[128,8,1024]{2,0,1:T(8,128)(2,1)} %bitcast.18), calls=%async_computation | async-start | bytes 4194304 | tf_op jit(solution)/shard_map/all_to_all | solution.py:168
  10.6 0.6 broadcast_in_dim.25
  11.2 0.6 convert_element_type.34.w_ref
  11.8 1.2 copy.31.xw_ref
  13.0 45.9 %all-to-all-done = bf16[128,8,1024]{2,0,1:T(8,128)(2,1)S(1)} async-done(((bf16[128,8,1024]{2,0,1:T(8,128)(2,1)}), bf16[128,8,1024]{2,0,1:T(8,128)(2,1)S(1)}, u32[]{:S(2)}, u32[]{:S(2)}) %all-to-all-start) | async-done | bytes 2097184 | tf_op jit(solution)/shard_map/all_to_all | solution.py:168
  58.8 0.7 broadcast_in_dim.19.halo_ref
  59.5 0.7 copy-done
  60.2 8.4 %conv_project.1 = (bf16[1024,1024]{1,0:T(8,128)(2,1)}, f32[1024,288]{1,0:T(8,128)}) custom-call(bf16[1024,1024]{1,0:T(8,128)(2,1)} %bitcast.17, f32[1,8,1024]{2,1,0:T(8,128)} %broadcast_in_dim.19.halo_ref, f32[4,1024]{1,0:T(4,128)} %convert_element_type.34.w_ref, f32[1,1024]{1,0:T(1,128)} %bitcast.22, bf16[1024,288]{1,0:T(8,128)(2,1)} %copy.31.xw_ref), custom_call_target="tpu_custom_call" | custom-call | tf_op jit(solution)/shard_map/conv_project/pallas_call | solution.py:41
  68.5 2.9 %copy.32 = f32[8,128,288]{1,2,0:T(8,128)} copy(f32[8,128,288]{2,1,0:T(8,128)} %bitcast.21) | data formatting | bytes 2359296 | tf_op jit(solution)/shard_map/reshape | solution.py:174
  71.5 3.8 %all-to-all-start.1 = ((f32[8,128,288]{1,2,0:T(8,128)}), f32[8,128,288]{1,2,0:T(8,128)S(1)}, u32[]{:S(2)}, u32[]{:S(2)}) async-start(f32[8,128,288]{1,2,0:T(8,128)} %copy.32), calls=%async_computation.1 | async-start | bytes 2359296 | tf_op jit(solution)/shard_map/all_to_all | solution.py:173
  75.3 0.6 reshape.28.rate_ref
  75.9 28.1 %all-to-all-done.1 = f32[8,128,288]{1,2,0:T(8,128)S(1)} async-done(((f32[8,128,288]{1,2,0:T(8,128)}), f32[8,128,288]{1,2,0:T(8,128)S(1)}, u32[]{:S(2)}, u32[]{:S(2)}) %all-to-all-start.1) | async-done | bytes 1179680 | tf_op jit(solution)/shard_map/all_to_all | solution.py:173
  104.6 32.2 %all_gather.3 = bf16[1024,320]{1,0:T(8,128)(2,1)S(1)} all-gather(bf16[128,320]{1,0:T(8,128)(2,1)S(1)} %pad_maximum_fusion), channel_id=1, replica_groups=mesh['seq'=8,'batch'=4] {'seq'}, dimensions={0}, use_global_device_ids=true | all-gather | bytes 737280 | tf_op jit(solution)/shard_map/all_gather | solution.py:187
  136.8 0.1 convert_add_fusion
  136.9 0.8 slice.22.nm_ref
  137.8 0.9 reshape.31.bc_ref
  138.7 0.6 broadcast_in_dim.24.h0_ref
  139.3 29.6 %selective_scan.1 = bf16[1024,1024]{1,0:T(8,128)(2,1)} custom-call(bf16[1024,1024]{1,0:T(8,128)(2,1)} %get-tuple-element.7.xc_ref, bf16[1024,256]{1,0:T(8,128)(2,1)} %slice.22.nm_ref, f32[8,1,4096]{2,1,0:T(1,128)} %reshape.31.bc_ref, bf16[256,1024]{1,0:T(8,128)(2,1)} %dtw_ref.1, f32[1,1024]{1,0:T(1,128)} %bitcast.23, f32[128,128]{1,0:T(8,128)} %reshape.28.rate_ref, ...), custom_call_target="tpu_custom_call" | custom-call | tf_op jit(solution)/shard_map/selective_scan/pallas_call | solution.py:117
  168.9 46.1 %all_to_all.37 = bf16[8,128,1024]{2,1,0:T(8,128)(2,1)S(1)} all-to-all(bf16[8,128,1024]{2,1,0:T(8,128)(2,1)} %bitcast.19), channel_id=1, replica_groups=mesh['seq'=8,'batch'=4] {'seq'}, dimensions={0} | all-to-all | bytes 4194304 | tf_op jit(solution)/shard_map/all_to_all | solution.py:195
  215.0 0.5 convert_bitcast_fusion
  215.5 0.3 copy.40
  215.8 1.3 copy-done.1
  217.0 2.5 %fusion.4 = bf16[128,8192]{1,0:T(8,128)(2,1)} fusion(f32[128,8192]{1,0:T(8,128)S(1)} %bitcast.16, bf16[128,8192]{1,0:T(8,128)(2,1)S(1)} %copy-done.1), kind=kLoop, calls=%fused_computation.7 | loop fusion | flops 7340032 | bytes 8388608 | tf_op jit(solution)/shard_map/convert_element_type | solution.py:196
  (23 shorter events, 0.6 us)
Async XLA Ops:
  3.1 7.5 %copy-start.5 = (bf16[1024]{0:T(1024)(128)(2,1)S(1)}, bf16[1024]{0:T(1024)(128)(2,1)}, u32[]{:S(2)}) copy-start(bf16[1024]{0:T(1024)(128)(2,1)} %param.13) | copy-start | bytes 6148
  3.2 8.0 %copy-start.4 = (bf16[4,1024]{1,0:T(4,128)(2,1)S(1)}, bf16[4,1024]{1,0:T(4,128)(2,1)}, u32[]{:S(2)}) copy-start(bf16[4,1024]{1,0:T(4,128)(2,1)} %param.12) | copy-start | bytes 24580
  3.2 8.6 %copy-start.2 = (bf16[1024,288]{0,1:T(8,128)(2,1)S(1)}, bf16[1024,288]{0,1:T(8,128)(2,1)}, u32[]{:S(2)}) copy-start(bf16[1024,288]{0,1:T(8,128)(2,1)} %param.14) | copy-start | bytes 1769476
  3.2 55.7 %all-to-all-start = ((bf16[128,8,1024]{2,0,1:T(8,128)(2,1)}), bf16[128,8,1024]{2,0,1:T(8,128)(2,1)S(1)}, u32[]{:S(2)}, u32[]{:S(2)}) async-start(bf16[128,8,1024]{2,0,1:T(8,128)(2,1)} %bitcast.18), calls=%async_computation | async-start | bytes 4194304 | tf_op jit(solution)/shard_map/all_to_all | solution.py:168
  58.8 1.3 copy-start
  68.5 6.7 %copy-start.3 = (f32[16,1024]{1,0:T(8,128)S(1)}, f32[16,1024]{1,0:T(8,128)}, u32[]{:S(2)}) copy-start(f32[16,1024]{1,0:T(8,128)} %param.18) | copy-start | bytes 196612
  71.5 33.0 %copy-start.6 = (f32[256]{0:T(256)S(1)}, f32[256]{0:T(256)}, u32[]{:S(2)}) copy-start(f32[256]{0:T(256)} %param.15) | copy-start | bytes 3076
  71.5 32.5 %all-to-all-start.1 = ((f32[8,128,288]{1,2,0:T(8,128)}), f32[8,128,288]{1,2,0:T(8,128)S(1)}, u32[]{:S(2)}, u32[]{:S(2)}) async-start(f32[8,128,288]{1,2,0:T(8,128)} %copy.32), calls=%async_computation.1 | async-start | bytes 2359296 | tf_op jit(solution)/shard_map/all_to_all | solution.py:173
  215.4 1.6 copy-start.1

commit v2 on v1

--- a/solution.py
+++ b/solution.py
@@ -5,6 +5,7 @@
 from jax import lax
 from jax.experimental import pallas as pl
 from jax.experimental.pallas import tpu as pltpu
+from jax.sharding import Mesh
 from jax.sharding import PartitionSpec as P
 
 LOG2E = 1.4426950408889634
@@ -61,15 +62,16 @@
     )(arrived, halo, weight.astype(jnp.float32), bias.astype(jnp.float32)[None, :], x_weight)
 
 
-def scan_kernel(
-    states, xc_ref, nm_ref, bc_ref, dtw_ref, dtb_ref, rate_ref, skip_ref, h0_ref, y_ref, st, dr, ys, hs
+def prepare_kernel(
+    states, xc_ref, nm_ref, bc_ref, dtw_ref, dtb_ref, rate_ref, st, dr, end_ref, sum_ref
 ):
     rows, chans = xc_ref.shape
     group = chans // 128
 
     @pl.when(pl.program_id(1) == 0)
     def _():
-        hs[...] = h0_ref[0]
+        end_ref[...] = jnp.zeros_like(end_ref)
+        sum_ref[...] = jnp.zeros_like(sum_ref)
 
     raw = jnp.dot(nm_ref[...], dtw_ref[...], preferred_element_type=jnp.float32) + dtb_ref[...]
     step = jnp.maximum(raw, 0.0) + jnp.log1p(jnp.exp(-jnp.abs(raw)))
@@ -77,6 +79,79 @@
     for j in range(group):
         st[pl.ds(j, rows, stride=group), :] = step[:, j * 128 : (j + 1) * 128]
         dr[pl.ds(j, rows, stride=group), :] = drive[:, j * 128 : (j + 1) * 128]
+
+    rates = [rate_ref[n * group : (n + 1) * group, :] for n in range(states)]
+
+    def advance(t, carry):
+        at = pl.ds(pl.multiple_of(t * group, group), group)
+        s = st[at, :]
+        d = dr[at, :]
+        base = t * (2 * states)
+        after = [
+            jnp.exp2(s * rates[n]) * carry[n] + bc_ref[0, 0, base + n] * d for n in range(states)
+        ]
+        return tuple(after) + (carry[states] + s,)
+
+    carry = tuple(end_ref[0, n * group : (n + 1) * group, :] for n in range(states))
+    carry = lax.fori_loop(0, rows, advance, carry + (sum_ref[0],), unroll=4)
+    for n in range(states):
+        end_ref[0, n * group : (n + 1) * group, :] = carry[n]
+    sum_ref[0] = carry[states]
+
+
+def prepare(xc, normed, bc, dt_weight, dt_bias, rate2, first, parts, steps, block):
+    chans = xc.shape[1]
+    states2 = bc.shape[2] // block
+    states = states2 // 2
+    group = chans // 128
+    rank = normed.shape[1]
+    whole = lambda p, i: (0, 0)
+    tile = lambda p, i: ((first + p) * steps + i, 0)
+    mine = lambda p, i: (p * steps + i, 0)
+    total = parts * steps * block
+    return pl.pallas_call(
+        functools.partial(prepare_kernel, states),
+        grid=(parts, steps),
+        in_specs=[
+            pl.BlockSpec((block, chans), tile),
+            pl.BlockSpec((block, rank), tile),
+            pl.BlockSpec(
+                (1, 1, block * states2),
+                lambda p, i: ((first + p) * steps + i, 0, 0),
+                memory_space=pltpu.SMEM,
+            ),
+            pl.BlockSpec((rank, chans), whole),
+            pl.BlockSpec((1, chans), whole),
+            pl.BlockSpec((states * group, 128), whole),
+        ],
+        out_specs=[
+            pl.BlockSpec((block * group, 128), mine),
+            pl.BlockSpec((block * group, 128), mine),
+            pl.BlockSpec((1, states * group, 128), lambda p, i: (p, 0, 0)),
+            pl.BlockSpec((1, group, 128), lambda p, i: (p, 0, 0)),
+        ],
+        out_shape=[
+            jax.ShapeDtypeStruct((total * group, 128), jnp.float32),
+            jax.ShapeDtypeStruct((total * group, 128), jnp.float32),
+            jax.ShapeDtypeStruct((parts, states * group, 128), jnp.float32),
+            jax.ShapeDtypeStruct((parts, group, 128), jnp.float32),
+        ],
+        cost_estimate=pl.CostEstimate(
+            flops=total * chans * (2 * rank + 5 * states),
+            bytes_accessed=total * chans * 10,
+            transcendentals=total * chans * states,
+        ),
+        name="prepare",
+    )(xc, normed, bc, dt_weight, dt_bias, rate2)
+
+
+def scan_kernel(states, xc_ref, st, dr, bc_ref, rate_ref, skip_ref, h0_ref, y_ref, ys, hs):
+    rows, chans = xc_ref.shape
+    group = chans // 128
+
+    @pl.when(pl.program_id(1) == 0)
+    def _():
+        hs[...] = h0_ref[0].astype(jnp.float32)
 
     rates = [rate_ref[n * group : (n + 1) * group, :] for n in range(states)]
 
@@ -105,52 +180,51 @@
         y_ref[:, sl] = y.astype(jnp.bfloat16)
 
 
-def scan(xc, normed, bc, dt_weight, dt_bias, rate2, skip, start, parts, block):
-    total, chans = xc.shape
-    states2 = bc.shape[1]
+def scan(xc, st, dr, bc, rate2, skip, start, first, parts, steps, block):
+    chans = xc.shape[1]
+    states2 = bc.shape[2] // block
     states = states2 // 2
     group = chans // 128
-    steps = total // parts // block
-    rank = normed.shape[1]
     whole = lambda p, i: (0, 0)
-    tile = lambda p, i: (p * steps + i, 0)
+    mine = lambda p, i: (p * steps + i, 0)
+    total = parts * steps * block
     return pl.pallas_call(
         functools.partial(scan_kernel, states),
         grid=(parts, steps),
         in_specs=[
-            pl.BlockSpec((block, chans), tile),
-            pl.BlockSpec((block, rank), tile),
+            pl.BlockSpec((block, chans), lambda p, i: ((first + p) * steps + i, 0)),
+            pl.BlockSpec((block * group, 128), mine),
+            pl.BlockSpec((block * group, 128), mine),
             pl.BlockSpec(
-                (1, 1, block * states2), lambda p, i: (p * steps + i, 0, 0), memory_space=pltpu.SMEM
+                (1, 1, block * states2),
+                lambda p, i: ((first + p) * steps + i, 0, 0),
+                memory_space=pltpu.SMEM,
             ),
-            pl.BlockSpec((rank, chans), whole),
-            pl.BlockSpec((1, chans), whole),
             pl.BlockSpec((states * group, 128), whole),
             pl.BlockSpec((1, chans), whole),
             pl.BlockSpec((1, states * group, 128), lambda p, i: (p, 0, 0)),
         ],
-        out_specs=pl.BlockSpec((block, chans), tile),
+        out_specs=pl.BlockSpec((block, chans), mine),
         out_shape=jax.ShapeDtypeStruct((total, chans), jnp.bfloat16),
         scratch_shapes=[
             pltpu.VMEM((block * group, 128), jnp.float32),
-            pltpu.VMEM((block * group, 128), jnp.float32),
-            pltpu.VMEM((block * group, 128), jnp.float32),
             pltpu.VMEM((states * group, 128), jnp.float32),
         ],
+        cost_estimate=pl.CostEstimate(
+            flops=total * chans * 7 * states,
+            bytes_accessed=total * chans * 12,
+            transcendentals=total * chans * states,
+        ),
         name="selective_scan",
-    )(
-        xc,
-        normed,
-        bc.reshape(parts * steps, 1, block * states2),
-        dt_weight,
-        dt_bias[None, :],
-        rate2.reshape(states * group, 128),
-        skip[None, :],
-        start,
-    )
+    )(xc, st, dr, bc, rate2, skip, start)
+
+
+PLANE = ("core", "x", "y")
+SPLITS = 2
 
 
 def local(
+    sizes,
     conv_input,
     gate_input,
     conv_weight,
@@ -162,16 +236,33 @@
     a_log,
     skip,
 ):
+    depth, parts = sizes
     rank, chans = dt_weight.shape
     states = a_log.shape[0]
     rows = conv_input.shape[0]
-    arrived = lax.all_to_all(conv_input, "seq", split_axis=1, concat_axis=0, tiled=True)
-    halo = jnp.zeros((1, HALO, chans), jnp.float32)
+    group = chans // 128
+    cores = parts // lax.axis_size("x")
+    place = lambda z, b: z * parts + b % (parts // cores) * cores + b // (parts // cores)
+    swap = [(place(a, b), place(b, a)) for a in range(depth) for b in range(parts)]
+    move = lambda v: lax.ppermute(v, ("z", "x", "core"), swap)
+    following = [(z, z + 1) for z in range(depth - 1)]
+    onward = lambda v: lax.ppermute(v, "z", following)
+
+    conv_pack = move(jnp.concatenate([conv_weight, conv_bias[None, :]], 0))
+    x_weight = move(x_weight)
+    dt_weight = move(dt_weight)
+    scan_pack = move(jnp.concatenate([a_log, dt_bias[None, :], skip[None, :]], 0))
+    width = conv_weight.shape[0]
+    conv_weight, conv_bias = conv_pack[:width], conv_pack[width]
+
+    arrived = lax.all_to_all(conv_input, PLANE, split_axis=1, concat_axis=0, tiled=True)
+    span = arrived.shape[0] // parts
+    halo = onward(arrived.reshape(parts, span, chans)[:, span - HALO :]).astype(jnp.float32)
     conv_out, partial_value = conv_project(
-        arrived, halo, conv_weight, conv_bias, x_weight, 1, rows
+        arrived, halo, conv_weight, conv_bias, x_weight, parts, rows
     )
     shares = lax.all_to_all(
-        partial_value.reshape(-1, rows, partial_value.shape[1]), "seq", split_axis=0, concat_axis=0
+        partial_value.reshape(-1, rows, partial_value.shape[1]), PLANE, split_axis=0, concat_axis=0
     )
     proj = jnp.sum(shares, axis=0)
     dt_low = proj[:, :rank]
@@ -184,36 +275,60 @@
     high = lax.reduce_precision(bc, 8, 7)
     low = (bc - high).astype(jnp.bfloat16)
     packed = jnp.concatenate([normed, high.astype(jnp.bfloat16), low], 1)
-    everyone = lax.all_gather(packed, "seq", axis=0, tiled=True)
+    everyone = lax.all_gather(packed, PLANE, axis=0, tiled=True)
     normed_all = everyone[:, :rank]
     bc_all = everyone[:, rank : rank + 2 * states].astype(jnp.float32) + everyone[
         :, rank + 2 * states :
     ].astype(jnp.float32)
-    rate2 = -jnp.exp(a_log) * LOG2E
-    start = jnp.zeros((1, states * chans // 128, 128), jnp.float32)
-    y_out = scan(conv_out, normed_all, bc_all, dt_weight, dt_bias, rate2, skip, start, 1, rows)
-    returned = lax.all_to_all(y_out, "seq", split_axis=0, concat_axis=1, tiled=True)
+    bc_all = bc_all.reshape(-1, 1, rows * 2 * states)
+    rate2 = (-jnp.exp(scan_pack[:states]) * LOG2E).reshape(states * group, 128)
+    dt_bias, skip = scan_pack[states : states + 1], scan_pack[states + 1 :]
+    steps = span // rows
+    some = parts // SPLITS
+    pieces = []
+    for first in range(0, parts, some):
+        st, dr, ends, sums = prepare(
+            conv_out, normed_all, bc_all, dt_weight, dt_bias, rate2, first, some, steps, rows
+        )
+        decay = jnp.exp2(
+            sums[:, None] * rate2.reshape(1, states, group, 128)
+        ).reshape(ends.shape)
+        start = onward(ends.astype(jnp.bfloat16))
+        for _ in range(depth - 2):
+            start = onward((decay * start.astype(jnp.float32) + ends).astype(jnp.bfloat16))
+        pieces.append(
+            scan(conv_out, st, dr, bc_all, rate2, skip, start, first, some, steps, rows)
+        )
+    y_out = jnp.concatenate(pieces, 0)
+    returned = lax.all_to_all(y_out, PLANE, split_axis=0, concat_axis=1, tiled=True)
     return (returned.astype(jnp.float32) * jax.nn.silu(gate_input.astype(jnp.float32))).astype(
         jnp.bfloat16
     )
 
 
 def solution(mesh):
+    seq, batch = mesh.shape["seq"], mesh.shape["batch"]
+    cores = 2
+    grid = Mesh(
+        mesh.devices.reshape(batch, seq // batch, batch // cores, cores), ("z", "y", "x", "core")
+    )
+    seqs = ("z", "y")
+    rows = P(("x", "core", "z", "y"), None)
     return jax.shard_map(
-        local,
-        mesh=mesh,
+        functools.partial(local, (batch, batch)),
+        mesh=grid,
         in_specs=(
-            P(("batch", "seq"), None),
-            P(("batch", "seq"), None),
-            P(None, "seq"),
-            P("seq"),
-            P("seq", None),
+            rows,
+            rows,
+            P(None, seqs),
+            P(seqs),
+            P(seqs, None),
             P(),
-            P(None, "seq"),
-            P("seq"),
-            P(None, "seq"),
-            P("seq"),
+            P(None, seqs),
+            P(seqs),
+            P(None, seqs),
+            P(seqs),
         ),
-        out_specs=P(("batch", "seq"), None),
+        out_specs=rows,
         check_vma=False,
     )

time: 220 us -> 245 us (1.11)
  starting transfers between devices: 11.2 us -> 39.3 us
  Pallas kernels: 37.9 us -> 61 us
  blocking collectives: 78.3 us -> 57.7 us
  waiting for transfers between devices: 74 us -> 61.3 us
  other arithmetic: 4.66 us -> 10.5 us
    ppermute x0 -> x11, starting transfers between devices: none -> 30.2 us  [the longest x7 27.5 us: local(): onward = lambda v: lax.ppermute(v, 'z', following)]
    pallas_call x0 -> x2, Pallas kernels: none -> 24.2 us  [prepare(): pl.pallas_call(functools.partial(prepare_kernel, states), grid=(parts, st...]
    all_to_all x1, blocking collectives: 46.1 us -> 28.7 us  [local(): lax.all_to_all(y_out, PLANE, split_axis=0, concat_axis=1, tiled=True)]
    all_to_all x2, waiting for transfers between devices: 74 us -> 59.2 us  [the longest x1 34.7 us: local(): lax.all_to_all(conv_input, PLANE, split_axis=1, concat_axis=0, tiled=True)]
    convert_element_type x0 -> x7, other arithmetic: none -> 5.06 us  [the longest x3 1.98 us: local(): (decay * start.astype(jnp.float32) + ends).astype(jnp.bfloat16)]
    all_gather x1, blocking collectives: 32.2 us -> 29 us  [local(): everyone = lax.all_gather(packed, PLANE, axis=0, tiled=True)]
    pallas_call x1 -> x2, Pallas kernels: 29.6 us -> 28.4 us  [scan(): pl.pallas_call(functools.partial(scan_kernel, states), grid=(parts, steps...]
  transfers between devices with their start and end apart: 2 -> 13, of which waited for: 2 -> 5; matrix products, arithmetic and copies ran while one was open for 1% -> 3% of each run, Pallas kernels for 0% -> 11%
where the time goes in v2:
time: 245 us; the launch traced here: 244 us
  waiting for transfers between devices  61.3 us (25%)
  Pallas kernels  61 us (25%)
  blocking collectives  57.7 us (24%)
  starting transfers between devices  39.3 us (16%)
  local copies, waits for them, and re-layouts  14.2 us (6%)
  other arithmetic  10.5 us (4%)
    all_to_all x1, waiting for transfers between devices, local(): lax.all_to_all(conv_input, PLANE, split_axis=1, concat_axis=0, tiled=True)  34.7 us
    all_gather x1, blocking collectives, local(): everyone = lax.all_gather(packed, PLANE, axis=0, tiled=True)  29 us
    all_to_all x1, blocking collectives, local(): lax.all_to_all(y_out, PLANE, split_axis=0, concat_axis=1, tiled=True)  28.7 us
    pallas_call x2, Pallas kernels, scan(): pl.pallas_call(functools.partial(scan_kernel, states), grid=(parts, steps...  28.4 us
    ppermute x7, starting transfers between devices, local(): onward = lambda v: lax.ppermute(v, 'z', following)  27.5 us
    all_to_all x1, waiting for transfers between devices, local(): lax.all_to_all(partial_value.reshape(-1, rows, partial_value.shape[1]), P...  24.5 us
    pallas_call x2, Pallas kernels, prepare(): pl.pallas_call(functools.partial(prepare_kernel, states), grid=(parts, st...  24.2 us
    pallas_call x1, Pallas kernels, conv_project(): pl.pallas_call(functools.partial(conv_kernel, width), grid=(parts, steps)...  8.45 us
  transfers between devices with their start and end apart: 13, of which 5 were waited for; matrix products, arithmetic and copies ran while one was open for 3% of the time, Pallas kernels for 11%

profile of v2, /device:TPU:0, one launch (start us, length us, event | category | flops | bytes accessed | tf_op | source)
XLA Modules:
  0.0 244.4 jit_solution(14112781972369339303)
XLA Ops:
  0.0 3.1 %copy.54 = bf16[16,8,8,1024]{3,2,0,1:T(8,128)(2,1)} copy(bf16[16,8,8,1024]{3,2,1,0:T(8,128)(2,1)} %bitcast.58) | data formatting | bytes 4194304 | tf_op jit(solution)/shard_map/all_to_all | solution.py:258
  3.2 5.3 %all-to-all-start = ((bf16[128,8,1024]{2,0,1:T(8,128)(2,1)}), bf16[128,8,1024]{2,0,1:T(8,128)(2,1)S(1)}, u32[]{:S(2)}, u32[]{:S(2)}) async-start(bf16[128,8,1024]{2,0,1:T(8,128)(2,1)} %bitcast.56), calls=%async_computation | async-start | bytes 4194304 | tf_op jit(solution)/shard_map/all_to_all | solution.py:258
  10.5 34.7 %all-to-all-done = bf16[128,8,1024]{2,0,1:T(8,128)(2,1)S(1)} async-done(((bf16[128,8,1024]{2,0,1:T(8,128)(2,1)}), bf16[128,8,1024]{2,0,1:T(8,128)(2,1)S(1)}, u32[]{:S(2)}, u32[]{:S(2)}) %all-to-all-start) | async-done | bytes 2097184 | tf_op jit(solution)/shard_map/all_to_all | solution.py:258
  45.2 5.7 %collective-permute-start = (bf16[4,8,1024]{2,1,0:T(8,128)(2,1)S(1)}, bf16[4,8,1024]{2,1,0:T(8,128)(2,1)S(1)}, u32[]{:S(2)}, u32[]{:S(2)}) collective-permute-start(bf16[4,8,1024]{2,1,0:T(8,128)(2,1)S(1)} %slice.44), channel_id=1, source_target_pairs={{0,8},{8,16},{16,24},{1,9},{9,17},{17,25},{2,10},{10,18},{18,26},{... | collective-permute-start | bytes 196616 | tf_op jit(solution)/shard_map/ppermute | solution.py:249
  53.5 8.4 %conv_project.1 = (bf16[1024,1024]{1,0:T(8,128)(2,1)}, f32[1024,288]{1,0:T(8,128)}) custom-call(bf16[1024,1024]{1,0:T(8,128)(2,1)} %bitcast.55, f32[4,8,1024]{2,1,0:T(8,128)} %convert_element_type.70.halo_ref, f32[4,1024]{1,0:T(4,128)} %slice_convert_fusion.w_ref, f32[1,1024]{1,0:T(1,128)} %slice_convert_fusion.1.b_ref, bf16[1024,288]{1,0:T(8,128)(2,1)} %copy.40.xw_ref), custom_call_target="tpu_custom_call" | custom-call | tf_op jit(solution)/shard_map/conv_project/pallas_call | solution.py:42
  62.0 3.0 %copy.41 = f32[8,128,288]{1,2,0:T(8,128)} copy(f32[8,128,288]{2,1,0:T(8,128)} %bitcast.59) | data formatting | bytes 2359296 | tf_op jit(solution)/shard_map/reshape | solution.py:265
  65.0 3.7 %all-to-all-start.1 = ((f32[8,128,288]{1,2,0:T(8,128)}), f32[8,128,288]{1,2,0:T(8,128)S(1)}, u32[]{:S(2)}, u32[]{:S(2)}) async-start(f32[8,128,288]{1,2,0:T(8,128)} %copy.41), calls=%async_computation.1 | async-start | bytes 2359296 | tf_op jit(solution)/shard_map/all_to_all | solution.py:264
  71.4 24.5 %all-to-all-done.1 = f32[8,128,288]{1,2,0:T(8,128)S(1)} async-done(((f32[8,128,288]{1,2,0:T(8,128)}), f32[8,128,288]{1,2,0:T(8,128)S(1)}, u32[]{:S(2)}, u32[]{:S(2)}) %all-to-all-start.1) | async-done | bytes 1179680 | tf_op jit(solution)/shard_map/all_to_all | solution.py:264
  96.5 29.0 %all_gather.3 = bf16[1024,320]{1,0:T(8,128)(2,1)S(1)} all-gather(bf16[128,320]{1,0:T(8,128)(2,1)S(1)} %pad_maximum_fusion.1), channel_id=1, replica_groups=mesh['z'=4,'y'=2,'x'=2,'core'=2] {'core','x','y'}, dimensions={0}, use_global_device_ids=true | all-gather | bytes 737280 | tf_op jit(solution)/shard_map/all_gather | solution.py:278
  128.3 12.1 %prepare.2 = (f32[4096,128]{1,0:T(8,128)}, f32[4096,128]{1,0:T(8,128)}, f32[2,128,128]{2,1,0:T(8,128)}, f32[2,8,128]{2,1,0:T(8,128)}) custom-call(bf16[1024,1024]{1,0:T(8,128)(2,1)} %get-tuple-element.15.xc_ref, bf16[1024,256]{1,0:T(8,128)(2,1)} %slice.49.nm_ref, f32[8,1,4096]{2,1,0:T(1,128)} %reshape.46.bc_ref, bf16[256,1024]{1,0:T(8,128)(2,1)} %copy-done.14, ...), custom_call_target="tpu_custom_call" | custom-call | flops 310378496 | bytes 5242880 | tf_op jit(solution)/shard_map/prepare/pallas_call | solution.py:112
  141.3 4.1 %collective-permute-start.5 = (bf16[2,128,128]{2,1,0:T(8,128)(2,1)S(1)}, bf16[2,128,128]{2,1,0:T(8,128)(2,1)S(1)}, u32[]{:S(2)}, u32[]{:S(2)}) collective-permute-start(bf16[2,128,128]{2,1,0:T(8,128)(2,1)S(1)} %convert_element_type.78), channel_id=1, source_target_pairs={{0,8},{8,16},{16,24},{1,9},{9,17},{17,25},{2,10},{10,18},{18,26},{... | collective-permute-start | bytes 196616 | tf_op jit(solution)/shard_map/ppermute | solution.py:249
  145.5 12.1 %prepare.3 = (f32[4096,128]{1,0:T(8,128)}, f32[4096,128]{1,0:T(8,128)}, f32[2,128,128]{2,1,0:T(8,128)}, f32[2,8,128]{2,1,0:T(8,128)}) custom-call(bf16[1024,1024]{1,0:T(8,128)(2,1)} %get-tuple-element.15.xc_ref, bf16[1024,256]{1,0:T(8,128)(2,1)} %slice.49.nm_ref, f32[8,1,4096]{2,1,0:T(1,128)} %reshape.46.bc_ref, bf16[256,1024]{1,0:T(8,128)(2,1)} %copy-done.14, ...), custom_call_target="tpu_custom_call" | custom-call | flops 310378496 | bytes 5242880 | tf_op jit(solution)/shard_map/prepare/pallas_call | solution.py:112
  158.5 3.8 %collective-permute-start.8 = (bf16[2,128,128]{2,1,0:T(8,128)(2,1)S(1)}, bf16[2,128,128]{2,1,0:T(8,128)(2,1)S(1)}, u32[]{:S(2)}, u32[]{:S(2)}) collective-permute-start(bf16[2,128,128]{2,1,0:T(8,128)(2,1)S(1)} %convert_element_type.83), channel_id=1, source_target_pairs={{0,8},{8,16},{16,24},{1,9},{9,17},{17,25},{2,10},{10,18},{18,26},{... | collective-permute-start | bytes 196616 | tf_op jit(solution)/shard_map/ppermute | solution.py:249
  162.3 3.2 %collective-permute-start.6 = (bf16[2,128,128]{2,1,0:T(8,128)(2,1)S(1)}, bf16[2,128,128]{2,1,0:T(8,128)(2,1)S(1)}, u32[]{:S(2)}, u32[]{:S(2)}) collective-permute-start(bf16[2,128,128]{2,1,0:T(8,128)(2,1)S(1)} %fusion.18), channel_id=1, source_target_pairs={{0,8},{8,16},{16,24},{1,9},{9,17},{17,25},{2,10},{10,18},{18,26},{... | collective-permute-start | bytes 196616 | tf_op jit(solution)/shard_map/ppermute | solution.py:249
  165.5 1.9 collective-permute-done.6
  168.4 4.3 %collective-permute-start.9 = (bf16[2,128,128]{2,1,0:T(8,128)(2,1)S(1)}, bf16[2,128,128]{2,1,0:T(8,128)(2,1)S(1)}, u32[]{:S(2)}, u32[]{:S(2)}) collective-permute-start(bf16[2,128,128]{2,1,0:T(8,128)(2,1)S(1)} %get-tuple-element.28), channel_id=1, source_target_pairs={{0,8},{8,16},{16,24},{1,9},{9,17},{17,25},{2,10},{10,18},{18,26},{... | collective-permute-start | bytes 196616 | tf_op jit(solution)/shard_map/ppermute | solution.py:249
  172.7 2.0 collective-permute-start.7
  175.7 4.4 %collective-permute-start.10 = (bf16[2,128,128]{2,1,0:T(8,128)(2,1)S(1)}, bf16[2,128,128]{2,1,0:T(8,128)(2,1)S(1)}, u32[]{:S(2)}, u32[]{:S(2)}) collective-permute-start(bf16[2,128,128]{2,1,0:T(8,128)(2,1)S(1)} %fusion.12), channel_id=1, source_target_pairs={{0,8},{8,16},{16,24},{1,9},{9,17},{17,25},{2,10},{10,18},{18,26},{... | collective-permute-start | bytes 196616 | tf_op jit(solution)/shard_map/ppermute | solution.py:249
  180.8 14.2 %selective_scan.2 = bf16[512,1024]{1,0:T(8,128)(2,1)} custom-call(bf16[1024,1024]{1,0:T(8,128)(2,1)} %get-tuple-element.15.xc_ref, f32[4096,128]{1,0:T(8,128)} %get-tuple-element.17.st, f32[4096,128]{1,0:T(8,128)} %get-tuple-element.18.dr, f32[8,1,4096]{2,1,0:T(1,128)} %reshape.46.bc_ref, f32[128,128]{1,0:T(8,128)} %reshape.44.rate_ref, ...), custom_call_target="tpu_custom_call" | custom-call | flops 58720256 | bytes 6291456 | tf_op jit(solution)/shard_map/selective_scan/pallas_call | solution.py:191
  195.6 14.2 %selective_scan.3 = bf16[512,1024]{1,0:T(8,128)(2,1)} custom-call(bf16[1024,1024]{1,0:T(8,128)(2,1)} %get-tuple-element.15.xc_ref, f32[4096,128]{1,0:T(8,128)} %get-tuple-element.21.st, f32[4096,128]{1,0:T(8,128)} %get-tuple-element.22.dr, f32[8,1,4096]{2,1,0:T(1,128)} %reshape.46.bc_ref, f32[128,128]{1,0:T(8,128)} %reshape.44.rate_ref, ...), custom_call_target="tpu_custom_call" | custom-call | flops 58720256 | bytes 6291456 | tf_op jit(solution)/shard_map/selective_scan/pallas_call | solution.py:191
  209.8 1.4 pad_maximum_fusion
  211.2 28.7 %all_to_all.37 = bf16[8,128,1024]{2,1,0:T(8,128)(2,1)S(1)} all-to-all(bf16[8,128,1024]{2,1,0:T(8,128)(2,1)S(1)} %bitcast.57), channel_id=1, replica_groups=mesh['z'=4,'y'=2,'x'=2,'core'=2] {'core','x','y'}, dimensions={0} | all-to-all | bytes 4194304 | tf_op jit(solution)/shard_map/all_to_all | solution.py:303
  240.7 1.3 copy-done.1
  242.0 2.5 %fusion.4 = bf16[128,8192]{1,0:T(8,128)(2,1)} fusion(f32[128,8192]{1,0:T(8,128)S(1)} %bitcast.53, bf16[128,8192]{1,0:T(8,128)(2,1)S(1)} %copy-done.1), kind=kLoop, calls=%fused_computation.7 | loop fusion | flops 7340032 | bytes 8388608 | tf_op jit(solution)/shard_map/convert_element_type | solution.py:304
  (78 shorter events, 16.4 us)
Async XLA Ops:
  3.2 6.1 %copy-start.7 = (bf16[4,1024]{1,0:T(4,128)(2,1)S(1)}, bf16[4,1024]{1,0:T(4,128)(2,1)}, u32[]{:S(2)}) copy-start(bf16[4,1024]{1,0:T(4,128)(2,1)} %param.12) | copy-start | bytes 24580
  3.2 42.0 %all-to-all-start = ((bf16[128,8,1024]{2,0,1:T(8,128)(2,1)}), bf16[128,8,1024]{2,0,1:T(8,128)(2,1)S(1)}, u32[]{:S(2)}, u32[]{:S(2)}) async-start(bf16[128,8,1024]{2,0,1:T(8,128)(2,1)} %bitcast.56), calls=%async_computation | async-start | bytes 4194304 | tf_op jit(solution)/shard_map/all_to_all | solution.py:258
  8.5 43.1 %collective-permute-start.2 = (bf16[1024,288]{0,1:T(8,128)(2,1)S(1)}, bf16[1024,288]{0,1:T(8,128)(2,1)S(1)}, u32[]{:S(2)}, u32[]{:S(2)}) collective-permute-start(bf16[1024,288]{0,1:T(8,128)(2,1)S(1)} %copy-done.12), channel_id=1, source_target_pairs={{0,0},{2,8},{1,16},{3,24},{8,2},{10,10},{9,18},{11,26},{16,1},{18,... | collective-permute-start | bytes 1769480 | tf_op jit(solution)/shard_map/ppermute | solution.py:247
  9.3 0.7 collective-permute-start.1
  45.2 8.3 %copy-start = (bf16[128,8,1024]{2,0,1:T(8,128)(2,1)}, bf16[128,8,1024]{2,0,1:T(8,128)(2,1)S(1)}, u32[]{:S(2)}) copy-start(bf16[128,8,1024]{2,0,1:T(8,128)(2,1)S(1)} %all-to-all-done) | copy-start | bytes 6291460
  45.2 7.6 %collective-permute-start = (bf16[4,8,1024]{2,1,0:T(8,128)(2,1)S(1)}, bf16[4,8,1024]{2,1,0:T(8,128)(2,1)S(1)}, u32[]{:S(2)}, u32[]{:S(2)}) collective-permute-start(bf16[4,8,1024]{2,1,0:T(8,128)(2,1)S(1)} %slice.44), channel_id=1, source_target_pairs={{0,8},{8,16},{16,24},{1,9},{9,17},{17,25},{2,10},{10,18},{18,26},{... | collective-permute-start | bytes 196616 | tf_op jit(solution)/shard_map/ppermute | solution.py:249
  62.0 6.7 %copy-start.5 = (f32[16,1024]{1,0:T(8,128)S(1)}, f32[16,1024]{1,0:T(8,128)}, u32[]{:S(2)}) copy-start(f32[16,1024]{1,0:T(8,128)} %param.18) | copy-start | bytes 196612
  62.0 6.7 %copy-start.8 = (f32[1024]{0:T(1024)S(1)}, f32[1024]{0:T(1024)}, u32[]{:S(2)}) copy-start(f32[1024]{0:T(1024)} %param.19) | copy-start | bytes 12292
  62.0 6.7 %copy-start.9 = (f32[1024]{0:T(1024)S(1)}, f32[1024]{0:T(1024)}, u32[]{:S(2)}) copy-start(f32[1024]{0:T(1024)} %param.17) | copy-start | bytes 12292
  62.0 7.4 %copy-start.13 = (bf16[256,1024]{1,0:T(8,128)(2,1)S(1)}, bf16[256,1024]{1,0:T(8,128)(2,1)}, u32[]{:S(2)}) copy-start(bf16[256,1024]{1,0:T(8,128)(2,1)} %param.16) | copy-start | bytes 1572868
  65.0 31.4 %copy-start.11 = (f32[256]{0:T(256)S(1)}, f32[256]{0:T(256)}, u32[]{:S(2)}) copy-start(f32[256]{0:T(256)} %param.15) | copy-start | bytes 3076
  65.0 30.9 %all-to-all-start.1 = ((f32[8,128,288]{1,2,0:T(8,128)}), f32[8,128,288]{1,2,0:T(8,128)S(1)}, u32[]{:S(2)}, u32[]{:S(2)}) async-start(f32[8,128,288]{1,2,0:T(8,128)} %copy.41), calls=%async_computation.1 | async-start | bytes 2359296 | tf_op jit(solution)/shard_map/all_to_all | solution.py:264
  68.7 1.4 collective-permute-start.4
  69.4 58.1 %collective-permute-start.3 = (bf16[256,1024]{1,0:T(8,128)(2,1)S(1)}, bf16[256,1024]{1,0:T(8,128)(2,1)S(1)}, u32[]{:S(2)}, u32[]{:S(2)}) collective-permute-start(bf16[256,1024]{1,0:T(8,128)(2,1)S(1)} %copy-done.13), channel_id=1, source_target_pairs={{0,0},{2,8},{1,16},{3,24},{8,2},{10,10},{9,18},{11,26},{16,1},{18,... | collective-permute-start | bytes 1572872 | tf_op jit(solution)/shard_map/ppermute | solution.py:247
  141.3 20.9 %copy-start.2 = (f32[2,128,128]{2,1,0:T(8,128)S(1)}, f32[2,128,128]{2,1,0:T(8,128)}, u32[]{:S(2)}) copy-start(f32[2,128,128]{2,1,0:T(8,128)} %get-tuple-element.20) | copy-start | bytes 393220
  141.3 20.9 %copy-start.3 = (f32[128,128]{1,0:T(8,128)S(1)}, f32[128,128]{1,0:T(8,128)}, u32[]{:S(2)}) copy-start(f32[128,128]{1,0:T(8,128)} %reshape.44.rate_ref) | copy-start | bytes 196612
  141.3 20.9 %copy-start.6 = (f32[2,8,128]{2,1,0:T(8,128)S(1)}, f32[2,8,128]{2,1,0:T(8,128)}, u32[]{:S(2)}) copy-start(f32[2,8,128]{2,1,0:T(8,128)} %get-tuple-element.19) | copy-start | bytes 24580
  141.3 20.9 %collective-permute-start.5 = (bf16[2,128,128]{2,1,0:T(8,128)(2,1)S(1)}, bf16[2,128,128]{2,1,0:T(8,128)(2,1)S(1)}, u32[]{:S(2)}, u32[]{:S(2)}) collective-permute-start(bf16[2,128,128]{2,1,0:T(8,128)(2,1)S(1)} %convert_element_type.78), channel_id=1, source_target_pairs={{0,8},{8,16},{16,24},{1,9},{9,17},{17,25},{2,10},{10,18},{18,26},{... | collective-permute-start | bytes 196616 | tf_op jit(solution)/shard_map/ppermute | solution.py:249
  158.5 7.1 %collective-permute-start.8 = (bf16[2,128,128]{2,1,0:T(8,128)(2,1)S(1)}, bf16[2,128,128]{2,1,0:T(8,128)(2,1)S(1)}, u32[]{:S(2)}, u32[]{:S(2)}) collective-permute-start(bf16[2,128,128]{2,1,0:T(8,128)(2,1)S(1)} %convert_element_type.83), channel_id=1, source_target_pairs={{0,8},{8,16},{16,24},{1,9},{9,17},{17,25},{2,10},{10,18},{18,26},{... | collective-permute-start | bytes 196616 | tf_op jit(solution)/shard_map/ppermute | solution.py:249
  162.3 5.1 %collective-permute-start.6 = (bf16[2,128,128]{2,1,0:T(8,128)(2,1)S(1)}, bf16[2,128,128]{2,1,0:T(8,128)(2,1)S(1)}, u32[]{:S(2)}, u32[]{:S(2)}) collective-permute-start(bf16[2,128,128]{2,1,0:T(8,128)(2,1)S(1)} %fusion.18), channel_id=1, source_target_pairs={{0,8},{8,16},{16,24},{1,9},{9,17},{17,25},{2,10},{10,18},{18,26},{... | collective-permute-start | bytes 196616 | tf_op jit(solution)/shard_map/ppermute | solution.py:249
  168.4 6.4 %collective-permute-start.9 = (bf16[2,128,128]{2,1,0:T(8,128)(2,1)S(1)}, bf16[2,128,128]{2,1,0:T(8,128)(2,1)S(1)}, u32[]{:S(2)}, u32[]{:S(2)}) collective-permute-start(bf16[2,128,128]{2,1,0:T(8,128)(2,1)S(1)} %get-tuple-element.28), channel_id=1, source_target_pairs={{0,8},{8,16},{16,24},{1,9},{9,17},{17,25},{2,10},{10,18},{18,26},{... | collective-permute-start | bytes 196616 | tf_op jit(solution)/shard_map/ppermute | solution.py:249
  172.7 7.5 %collective-permute-start.7 = (bf16[2,128,128]{2,1,0:T(8,128)(2,1)S(1)}, bf16[2,128,128]{2,1,0:T(8,128)(2,1)S(1)}, u32[]{:S(2)}, u32[]{:S(2)}) collective-permute-start(bf16[2,128,128]{2,1,0:T(8,128)(2,1)S(1)} %get-tuple-element.27), channel_id=1, source_target_pairs={{0,8},{8,16},{16,24},{1,9},{9,17},{17,25},{2,10},{10,18},{18,26},{... | collective-permute-start | bytes 196616 | tf_op jit(solution)/shard_map/ppermute | solution.py:249
  175.7 19.2 %collective-permute-start.10 = (bf16[2,128,128]{2,1,0:T(8,128)(2,1)S(1)}, bf16[2,128,128]{2,1,0:T(8,128)(2,1)S(1)}, u32[]{:S(2)}, u32[]{:S(2)}) collective-permute-start(bf16[2,128,128]{2,1,0:T(8,128)(2,1)S(1)} %fusion.12), channel_id=1, source_target_pairs={{0,8},{8,16},{16,24},{1,9},{9,17},{17,25},{2,10},{10,18},{18,26},{... | collective-permute-start | bytes 196616 | tf_op jit(solution)/shard_map/ppermute | solution.py:249
  195.6 14.2 %copy-start.4 = (bf16[512,1024]{1,0:T(8,128)(2,1)S(1)}, bf16[512,1024]{1,0:T(8,128)(2,1)}, u32[]{:S(2)}) copy-start(bf16[512,1024]{1,0:T(8,128)(2,1)} %selective_scan.2) | copy-start | bytes 3145732
  (6 other events, 15.0 us)

commit v3 on v2

--- a/solution.py
+++ b/solution.py
@@ -12,7 +12,101 @@
 HALO = 8
 
 
-def conv_kernel(width, x_ref, halo_ref, w_ref, b_ref, xw_ref, xc_ref, part_ref, prev):
+MESH = pl.DeviceIdType.MESH
+
+
+def pack(wide, exact):
+    high = exact.astype(jnp.bfloat16)
+    low = (exact - high.astype(jnp.float32)).astype(jnp.bfloat16)
+    rest = -(2 * exact.shape[1]) % 128
+    pieces = [wide.astype(jnp.bfloat16), high, low]
+    if rest:
+        pieces.append(jnp.zeros((exact.shape[0], rest), jnp.bfloat16))
+    return jnp.concatenate(pieces, 1)
+
+
+def place():
+    x, y, core = lax.axis_index("x"), lax.axis_index("y"), lax.axis_index("core")
+    return (core * lax.axis_size("x") + x) * lax.axis_size("y") + y
+
+
+def device(index):
+    ys, xs = lax.axis_size("y"), lax.axis_size("x")
+    part = index // ys
+    return {"x": lax.rem(part, xs), "y": lax.rem(index, ys), "core": part // xs}
+
+
+def greet(peers):
+    me = place()
+    barrier = pltpu.get_barrier_semaphore()
+    for k in range(1, peers):
+        pl.semaphore_signal(
+            barrier, inc=1, device_id=device(lax.rem(me + k, peers)), device_id_type=MESH
+        )
+    pl.semaphore_wait(barrier, peers - 1)
+    return me
+
+
+def reduce_kernel(peers, rank, states2, part_ref, gain_ref, out_ref, got, send_sem, recv_sem):
+    rows = got.shape[1]
+    me = greet(peers)
+    spread = []
+    for k in range(1, peers):
+        other = lax.rem(me + k, peers)
+        copy = pltpu.make_async_remote_copy(
+            src_ref=part_ref.at[pl.ds(pl.multiple_of(other * rows, rows), rows)],
+            dst_ref=got.at[k],
+            send_sem=send_sem.at[0, k],
+            recv_sem=recv_sem.at[0, k],
+            device_id=device(other),
+            device_id_type=MESH,
+        )
+        copy.start()
+        spread.append(copy)
+    mine = pl.ds(pl.multiple_of(me * rows, rows), rows)
+    total = part_ref[mine, :].astype(jnp.float32)
+    for k in range(1, peers):
+        spread[k - 1].wait_recv()
+        total = total + got[k].astype(jnp.float32)
+    low = total[:, :rank]
+    exact = total[:, rank : rank + states2] + total[:, rank + states2 : rank + 2 * states2]
+    normed = low * lax.rsqrt(jnp.mean(low * low, axis=1, keepdims=True) + 1e-06) * gain_ref[...]
+    out_ref[mine, :] = pack(normed, exact)
+    gather = []
+    for k in range(1, peers):
+        copy = pltpu.make_async_remote_copy(
+            src_ref=out_ref.at[mine],
+            dst_ref=out_ref.at[mine],
+            send_sem=send_sem.at[1, k],
+            recv_sem=recv_sem.at[1, k],
+            device_id=device(lax.rem(me + k, peers)),
+            device_id_type=MESH,
+        )
+        copy.start()
+        gather.append(copy)
+    for k in range(1, peers):
+        spread[k - 1].wait_send()
+        gather[k - 1].wait()
+
+
+def reduce_norm(partial, gain, peers, rank, states2):
+    total, cols = partial.shape
+    return pl.pallas_call(
+        functools.partial(reduce_kernel, peers, rank, states2),
+        in_specs=[pl.BlockSpec(memory_space=pltpu.VMEM)] * 2,
+        out_specs=pl.BlockSpec(memory_space=pltpu.VMEM),
+        out_shape=jax.ShapeDtypeStruct((total, cols), jnp.bfloat16),
+        scratch_shapes=[
+            pltpu.VMEM((peers, total // peers, cols), jnp.bfloat16),
+            pltpu.SemaphoreType.DMA((2, peers)),
+            pltpu.SemaphoreType.DMA((2, peers)),
+        ],
+        compiler_params=pltpu.CompilerParams(collective_id=0, has_side_effects=True),
+        name="reduce_norm",
+    )(partial, gain[None, :])
+
+
+def conv_kernel(width, rank, x_ref, halo_ref, w_ref, b_ref, xw_ref, xc_ref, part_ref, prev):
     rows, chans = x_ref.shape
     chunk = min(chans, 256)
 
@@ -30,17 +124,19 @@
             total = total + w_ref[tap : tap + 1, sl] * ext[low : low + rows]
         xc_ref[:, sl] = (total / (1.0 + jnp.exp(-total))).astype(jnp.bfloat16)
         prev[:, sl] = cur[rows - HALO :]
-    part_ref[...] = jnp.dot(xc_ref[...], xw_ref[...], preferred_element_type=jnp.float32)
-
-
-def conv_project(arrived, halo, weight, bias, x_weight, parts, block):
+    part = jnp.dot(xc_ref[...], xw_ref[...], preferred_element_type=jnp.float32)
+    part_ref[...] = pack(part[:, :rank], part[:, rank:])
+
+
+def conv_project(arrived, halo, weight, bias, x_weight, parts, block, rank):
     total, chans = arrived.shape
     steps = total // parts // block
     cols = x_weight.shape[1]
     width = weight.shape[0]
+    packed = rank + -(-2 * (cols - rank) // 128) * 128
     whole = lambda p, i: (0, 0)
     return pl.pallas_call(
-        functools.partial(conv_kernel, width),
+        functools.partial(conv_kernel, width, rank),
         grid=(parts, steps),
         in_specs=[
             pl.BlockSpec((block, chans), lambda p, i: (p * steps + i, 0)),
@@ -51,11 +147,11 @@
         ],
         out_specs=[
             pl.BlockSpec((block, chans), lambda p, i: (p * steps + i, 0)),
-            pl.BlockSpec((block, cols), lambda p, i: (p * steps + i, 0)),
+            pl.BlockSpec((block, packed), lambda p, i: (p * steps + i, 0)),
         ],
         out_shape=[
             jax.ShapeDtypeStruct((total, chans), jnp.bfloat16),
-            jax.ShapeDtypeStruct((total, cols), jnp.float32),
+            jax.ShapeDtypeStruct((total, packed), jnp.bfloat16),
         ],
         scratch_shapes=[pltpu.VMEM((HALO, chans), jnp.float32)],
         name="conv_project",
@@ -145,82 +241,110 @@
     )(xc, normed, bc, dt_weight, dt_bias, rate2)
 
 
-def scan_kernel(states, xc_ref, st, dr, bc_ref, rate_ref, skip_ref, h0_ref, y_ref, ys, hs):
-    rows, chans = xc_ref.shape
+def scan_kernel(
+    states, parts, peers, xc_ref, st, dr, bc_ref, rate_ref, skip_ref, h0_ref, out_ref,
+    ybuf, ys, hs, send_sem, recv_sem, own_sem,
+):
+    total, chans = xc_ref.shape
     group = chans // 128
-
-    @pl.when(pl.program_id(1) == 0)
-    def _():
-        hs[...] = h0_ref[0].astype(jnp.float32)
-
+    rows = total // peers
+    steps = total // parts // rows
+    xs = lax.axis_size("x")
+    cores = parts // xs
+    x = lax.axis_index("x")
+    me = greet(peers)
+    columns = out_ref.at[:, pl.ds(pl.multiple_of(me * chans, chans), chans)]
     rates = [rate_ref[n * group : (n + 1) * group, :] for n in range(states)]
 
-    def advance(t, hidden):
-        at = pl.ds(pl.multiple_of(t * group, group), group)
-        s = st[at, :]
-        d = dr[at, :]
-        base = t * (2 * states)
-        after = []
-        sums = [None, None]
+    def send(block):
+        away = lax.rem(block - me + peers, peers)
+        return pltpu.make_async_remote_copy(
+            src_ref=ybuf.at[block],
+            dst_ref=columns,
+            send_sem=send_sem.at[away],
+            recv_sem=recv_sem.at[away],
+            device_id=device(block),
+            device_id_type=MESH,
+        )
+
+    own = pltpu.make_async_copy(ybuf.at[me], columns, own_sem)
+
+    def one_block(place_in_order, _):
+        turn, i = place_in_order // steps, lax.rem(place_in_order, steps)
+        part = lax.rem(turn, cores) * xs + lax.rem(x + 1 + turn // cores, xs)
+        block = part * steps + i
+        base_row = pl.multiple_of(block * rows, rows)
+
+        @pl.when(i == 0)
+        def _():
+            hs[...] = h0_ref[part].astype(jnp.float32)
+
+        def advance(t, hidden):
+            at = pl.ds(pl.multiple_of((base_row + t) * group, group), group)
+            s = st[at, :]
+            d = dr[at, :]
+            base = (base_row + t) * (2 * states)
+            after = []
+            sums = [None, None]
+            for n in range(states):
+                h = jnp.exp2(s * rates[n]) * hidden[n] + bc_ref[base + n] * d
+                after.append(h)
+                term = bc_ref[base + states + n] * h
+                sums[n % 2] = term if sums[n % 2] is None else sums[n % 2] + term
+            ys[pl.ds(pl.multiple_of(t * group, group), group), :] = sums[0] + sums[1]
+            return tuple(after)
+
+        hidden = tuple(hs[n * group : (n + 1) * group, :] for n in range(states))
+        hidden = lax.fori_loop(0, rows, advance, hidden, unroll=4)
         for n in range(states):
-            h = jnp.exp2(s * rates[n]) * hidden[n] + bc_ref[0, 0, base + n] * d
-            after.append(h)
-            term = bc_ref[0, 0, base + states + n] * h
-            sums[n % 2] = term if sums[n % 2] is None else sums[n % 2] + term
-        ys[at, :] = sums[0] + sums[1]
-        return tuple(after)
-
-    hidden = tuple(hs[n * group : (n + 1) * group, :] for n in range(states))
-    hidden = lax.fori_loop(0, rows, advance, hidden, unroll=4)
-    for n in range(states):
-        hs[n * group : (n + 1) * group, :] = hidden[n]
-    for j in range(group):
-        sl = slice(j * 128, (j + 1) * 128)
-        y = ys[pl.ds(j, rows, stride=group), :] + skip_ref[:, sl] * xc_ref[:, sl].astype(jnp.float32)
-        y_ref[:, sl] = y.astype(jnp.bfloat16)
-
-
-def scan(xc, st, dr, bc, rate2, skip, start, first, parts, steps, block):
-    chans = xc.shape[1]
-    states2 = bc.shape[2] // block
-    states = states2 // 2
+            hs[n * group : (n + 1) * group, :] = hidden[n]
+        for j in range(group):
+            sl = slice(j * 128, (j + 1) * 128)
+            skipped = skip_ref[:, sl] * xc_ref[pl.ds(base_row, rows), sl].astype(jnp.float32)
+            y = ys[pl.ds(j, rows, stride=group), :] + skipped
+            ybuf[block, :, sl] = y.astype(jnp.bfloat16)
+
+        @pl.when(block == me)
+        def _():
+            own.start()
+
+        @pl.when(block != me)
+        def _():
+            send(block).start()
+
+        return 0
+
+    lax.fori_loop(0, peers, one_block, 0)
+    own.wait()
+    for k in range(1, peers):
+        send(lax.rem(me + k, peers)).wait()
+
+
+def scan(xc, st, dr, bc, rate2, skip, start, parts, peers):
+    total, chans = xc.shape
+    states = bc.shape[0] // total // 2
     group = chans // 128
-    whole = lambda p, i: (0, 0)
-    mine = lambda p, i: (p * steps + i, 0)
-    total = parts * steps * block
+    rows = total // peers
+    vmem = pl.BlockSpec(memory_space=pltpu.VMEM)
     return pl.pallas_call(
-        functools.partial(scan_kernel, states),
-        grid=(parts, steps),
-        in_specs=[
-            pl.BlockSpec((block, chans), lambda p, i: ((first + p) * steps + i, 0)),
-            pl.BlockSpec((block * group, 128), mine),
-            pl.BlockSpec((block * group, 128), mine),
-            pl.BlockSpec(
-                (1, 1, block * states2),
-                lambda p, i: ((first + p) * steps + i, 0, 0),
-                memory_space=pltpu.SMEM,
-            ),
-            pl.BlockSpec((states * group, 128), whole),
-            pl.BlockSpec((1, chans), whole),
-            pl.BlockSpec((1, states * group, 128), lambda p, i: (p, 0, 0)),
-        ],
-        out_specs=pl.BlockSpec((block, chans), mine),
-        out_shape=jax.ShapeDtypeStruct((total, chans), jnp.bfloat16),
+        functools.partial(scan_kernel, states, parts, peers),
+        in_specs=[vmem, vmem, vmem, pl.BlockSpec(memory_space=pltpu.SMEM), vmem, vmem, vmem],
+        out_specs=pl.BlockSpec(memory_space=pl.ANY),
+        out_shape=jax.ShapeDtypeStruct((rows, peers * chans), jnp.bfloat16),
         scratch_shapes=[
-            pltpu.VMEM((block * group, 128), jnp.float32),
+            pltpu.VMEM((peers, rows, chans), jnp.bfloat16),
+            pltpu.VMEM((rows * group, 128), jnp.float32),
             pltpu.VMEM((states * group, 128), jnp.float32),
-        ],
-        cost_estimate=pl.CostEstimate(
-            flops=total * chans * 7 * states,
-            bytes_accessed=total * chans * 12,
-            transcendentals=total * chans * states,
-        ),
+            pltpu.SemaphoreType.DMA((peers,)),
+            pltpu.SemaphoreType.DMA((peers,)),
+            pltpu.SemaphoreType.DMA,
+        ],
+        compiler_params=pltpu.CompilerParams(collective_id=1, has_side_effects=True),
         name="selective_scan",
     )(xc, st, dr, bc, rate2, skip, start)
 
 
 PLANE = ("core", "x", "y")
-SPLITS = 2
 
 
 def local(
@@ -259,48 +383,27 @@
     span = arrived.shape[0] // parts
     halo = onward(arrived.reshape(parts, span, chans)[:, span - HALO :]).astype(jnp.float32)
     conv_out, partial_value = conv_project(
-        arrived, halo, conv_weight, conv_bias, x_weight, parts, rows
-    )
-    shares = lax.all_to_all(
-        partial_value.reshape(-1, rows, partial_value.shape[1]), PLANE, split_axis=0, concat_axis=0
-    )
-    proj = jnp.sum(shares, axis=0)
-    dt_low = proj[:, :rank]
-    bc = proj[:, rank:]
-    normed = (
-        dt_low
-        * lax.rsqrt(jnp.mean(dt_low * dt_low, axis=1, keepdims=True) + 1e-06)
-        * dt_gain[None, :]
-    ).astype(jnp.bfloat16)
-    high = lax.reduce_precision(bc, 8, 7)
-    low = (bc - high).astype(jnp.bfloat16)
-    packed = jnp.concatenate([normed, high.astype(jnp.bfloat16), low], 1)
-    everyone = lax.all_gather(packed, PLANE, axis=0, tiled=True)
+        arrived, halo, conv_weight, conv_bias, x_weight, parts, rows, rank
+    )
+    everyone = reduce_norm(partial_value, dt_gain, arrived.shape[0] // rows, rank, 2 * states)
     normed_all = everyone[:, :rank]
     bc_all = everyone[:, rank : rank + 2 * states].astype(jnp.float32) + everyone[
-        :, rank + 2 * states :
+        :, rank + 2 * states : rank + 4 * states
     ].astype(jnp.float32)
     bc_all = bc_all.reshape(-1, 1, rows * 2 * states)
     rate2 = (-jnp.exp(scan_pack[:states]) * LOG2E).reshape(states * group, 128)
     dt_bias, skip = scan_pack[states : states + 1], scan_pack[states + 1 :]
     steps = span // rows
-    some = parts // SPLITS
-    pieces = []
-    for first in range(0, parts, some):
-        st, dr, ends, sums = prepare(
-            conv_out, normed_all, bc_all, dt_weight, dt_bias, rate2, first, some, steps, rows
-        )
-        decay = jnp.exp2(
-            sums[:, None] * rate2.reshape(1, states, group, 128)
-        ).reshape(ends.shape)
-        start = onward(ends.astype(jnp.bfloat16))
-        for _ in range(depth - 2):
-            start = onward((decay * start.astype(jnp.float32) + ends).astype(jnp.bfloat16))
-        pieces.append(
-            scan(conv_out, st, dr, bc_all, rate2, skip, start, first, some, steps, rows)
-        )
-    y_out = jnp.concatenate(pieces, 0)
-    returned = lax.all_to_all(y_out, PLANE, split_axis=0, concat_axis=1, tiled=True)
+    st, dr, ends, sums = prepare(
+        conv_out, normed_all, bc_all, dt_weight, dt_bias, rate2, 0, parts, steps, rows
+    )
+    decay = jnp.exp2(sums[:, None] * rate2.reshape(1, states, group, 128)).reshape(ends.shape)
+    start = onward(ends.astype(jnp.bfloat16))
+    for _ in range(depth - 2):
+        start = onward((decay * start.astype(jnp.float32) + ends).astype(jnp.bfloat16))
+    returned = scan(
+        conv_out, st, dr, bc_all.reshape(-1), rate2, skip, start, parts, arrived.shape[0] // rows
+    )
     return (returned.astype(jnp.float32) * jax.nn.silu(gate_input.astype(jnp.float32))).astype(
         jnp.bfloat16
     )

time: 245 us -> 197 us (0.80)
  blocking collectives: 57.7 us -> 0 us
  Pallas kernels: 61 us -> 96.6 us
  starting transfers between devices: 39.3 us -> 28 us
  waiting for transfers between devices: 61.3 us -> 50.9 us
  local copies, waits for them, and re-layouts: 14.2 us -> 9.98 us
    pallas_call x3, Pallas kernels: 36.9 us -> 74.6 us  [the longest x1 41.7 us: scan(): pl.pallas_call(functools.partial(scan_kernel, states, parts, peers), in_s...]
    all_gather x1 -> x0, blocking collectives: 29 us -> none  [local(): everyone = lax.all_gather(packed, PLANE, axis=0, tiled=True)]
    all_to_all x1 -> x0, blocking collectives: 28.7 us -> none  [local(): lax.all_to_all(y_out, PLANE, split_axis=0, concat_axis=1, tiled=True)]
    all_to_all x1 -> x0, waiting for transfers between devices: 24.5 us -> none  [local(): lax.all_to_all(partial_value.reshape(-1, rows, partial_value.shape[1]), P...]
    all_to_all x1, waiting for transfers between devices: 34.7 us -> 44.2 us  [local(): lax.all_to_all(conv_input, PLANE, split_axis=1, concat_axis=0, tiled=True)]
    ppermute x7 -> x4, starting transfers between devices: 27.5 us -> 18.3 us  [local(): onward = lambda v: lax.ppermute(v, 'z', following)]
    ppermute x7 -> x4, waiting for transfers between devices: 2.08 us -> 6.67 us  [local(): onward = lambda v: lax.ppermute(v, 'z', following)]
    all_to_all x1 -> x0, starting transfers between devices: 3.7 us -> none  [local(): lax.all_to_all(partial_value.reshape(-1, rows, partial_value.shape[1]), P...]
  transfers between devices with their start and end apart: 13 -> 9, of which waited for: 5 -> 4; matrix products, arithmetic and copies ran while one was open for 3% -> 5% of each run, Pallas kernels for 11% -> 17%
where the time goes in v3:
time: 197 us; the launch traced here: 196 us
  Pallas kernels  96.6 us (49%)
  waiting for transfers between devices  50.9 us (26%)
  starting transfers between devices  28 us (14%)
  other arithmetic  10.4 us (5%)
  local copies, waits for them, and re-layouts  9.98 us (5%)
    all_to_all x1, waiting for transfers between devices, local(): lax.all_to_all(conv_input, PLANE, split_axis=1, concat_axis=0, tiled=True)  44.2 us
    pallas_call x1, Pallas kernels, scan(): pl.pallas_call(functools.partial(scan_kernel, states, parts, peers), in_s...  41.7 us
    pallas_call x1, Pallas kernels, reduce_norm(): pl.pallas_call(functools.partial(reduce_kernel, peers, rank, states2), in...  24.3 us
    pallas_call x1, Pallas kernels, prepare(): pl.pallas_call(functools.partial(prepare_kernel, states), grid=(parts, st...  22 us
    ppermute x4, starting transfers between devices, local(): onward = lambda v: lax.ppermute(v, 'z', following)  18.3 us
    pallas_call x1, Pallas kernels, conv_project(): pl.pallas_call(functools.partial(conv_kernel, width, rank), grid=(parts,...  8.63 us
    ppermute x4, waiting for transfers between devices, local(): onward = lambda v: lax.ppermute(v, 'z', following)  6.67 us
    all_to_all x1, starting transfers between devices, local(): lax.all_to_all(conv_input, PLANE, split_axis=1, concat_axis=0, tiled=True)  5.21 us
  transfers between devices with their start and end apart: 9, of which 4 were waited for; matrix products, arithmetic and copies ran while one was open for 5% of the time, Pallas kernels for 17%

profile of v3, /device:TPU:0, one launch (start us, length us, event | category | flops | bytes accessed | tf_op | source)
XLA Modules:
  0.0 196.0 jit_solution(6166070009690305414)
XLA Ops:
  0.0 3.2 %copy.21 = bf16[16,8,8,1024]{3,2,0,1:T(8,128)(2,1)} copy(bf16[16,8,8,1024]{3,2,1,0:T(8,128)(2,1)} %bitcast.33) | data formatting | bytes 4194304 | tf_op jit(solution)/shard_map/all_to_all | solution.py:382
  3.3 5.2 %all-to-all-start = ((bf16[128,8,1024]{2,0,1:T(8,128)(2,1)}), bf16[128,8,1024]{2,0,1:T(8,128)(2,1)S(1)}, u32[]{:S(2)}, u32[]{:S(2)}) async-start(bf16[128,8,1024]{2,0,1:T(8,128)(2,1)} %bitcast.32), calls=%async_computation | async-start | bytes 4194304 | tf_op jit(solution)/shard_map/all_to_all | solution.py:382
  9.9 1.5 collective-permute-start.3
  11.4 1.7 collective-permute-start.2
  14.3 44.2 %all-to-all-done = bf16[128,8,1024]{2,0,1:T(8,128)(2,1)S(1)} async-done(((bf16[128,8,1024]{2,0,1:T(8,128)(2,1)}), bf16[128,8,1024]{2,0,1:T(8,128)(2,1)S(1)}, u32[]{:S(2)}, u32[]{:S(2)}) %all-to-all-start) | async-done | bytes 2097184 | tf_op jit(solution)/shard_map/all_to_all | solution.py:382
  58.6 5.7 %collective-permute-start = (bf16[4,8,1024]{2,1,0:T(8,128)(2,1)S(1)}, bf16[4,8,1024]{2,1,0:T(8,128)(2,1)S(1)}, u32[]{:S(2)}, u32[]{:S(2)}) collective-permute-start(bf16[4,8,1024]{2,1,0:T(8,128)(2,1)S(1)} %slice.36), channel_id=1, source_target_pairs={{0,8},{8,16},{16,24},{1,9},{9,17},{17,25},{2,10},{10,18},{18,26},{... | collective-permute-start | bytes 196616 | tf_op jit(solution)/shard_map/ppermute | solution.py:373
  65.5 1.2 copy.17.xw_ref
  67.4 8.6 %conv_project.1 = (bf16[1024,1024]{1,0:T(8,128)(2,1)}, bf16[1024,384]{1,0:T(8,128)(2,1)}) custom-call(bf16[1024,1024]{1,0:T(8,128)(2,1)} %bitcast.31, f32[4,8,1024]{2,1,0:T(8,128)} %convert_element_type.40.halo_ref, f32[4,1024]{1,0:T(4,128)} %slice_convert_fusion.w_ref, f32[1,1024]{1,0:T(1,128)} %slice_convert_fusion.1.b_ref, bf16[1024,288]{1,0:T(8,128)(2,1)} %copy.17.xw_ref), custom_call_target="tpu_custom_call" | custom-call | tf_op jit(solution)/shard_map/conv_project/pallas_call | solution.py:138
  76.0 24.3 %reduce_norm.1 = bf16[1024,384]{1,0:T(8,128)(2,1)} custom-call(bf16[1024,384]{1,0:T(8,128)(2,1)} %get-tuple-element.12.part_ref, f32[1,256]{1,0:T(1,128)} %bitcast.36), custom_call_target="tpu_custom_call" | custom-call | tf_op jit(solution)/shard_map/reduce_norm/pallas_call | solution.py:94
  100.3 1.9 slice.30.nm_ref
  102.2 1.2 convert_add_fusion
  103.4 0.9 reshape.22.bc_ref
  104.3 22.0 %prepare.1 = (f32[8192,128]{1,0:T(8,128)}, f32[8192,128]{1,0:T(8,128)}, f32[4,128,128]{2,1,0:T(8,128)}, f32[4,8,128]{2,1,0:T(8,128)}) custom-call(bf16[1024,1024]{1,0:T(8,128)(2,1)} %get-tuple-element.11.xc_ref, bf16[1024,256]{1,0:T(8,128)(2,1)} %slice.30.nm_ref, f32[8,1,4096]{2,1,0:T(1,128)} %reshape.22.bc_ref, ...), custom_call_target="tpu_custom_call" | custom-call | flops 620756992 | bytes 10485760 | tf_op jit(solution)/shard_map/prepare/pallas_call | solution.py:208
  126.3 1.0 convert_element_type.45
  127.3 3.8 %collective-permute-start.5 = (bf16[4,128,128]{2,1,0:T(8,128)(2,1)S(1)}, bf16[4,128,128]{2,1,0:T(8,128)(2,1)S(1)}, u32[]{:S(2)}, u32[]{:S(2)}) collective-permute-start(bf16[4,128,128]{2,1,0:T(8,128)(2,1)S(1)} %convert_element_type.45), channel_id=1, source_target_pairs={{0,8},{8,16},{16,24},{1,9},{9,17},{17,25},{2,10},{10,18},{18,26},{... | collective-permute-start | bytes 393224 | tf_op jit(solution)/shard_map/ppermute | solution.py:373
  131.1 2.5 %collective-permute-done.5 = bf16[4,128,128]{2,1,0:T(8,128)(2,1)S(1)} collective-permute-done((bf16[4,128,128]{2,1,0:T(8,128)(2,1)S(1)}, bf16[4,128,128]{2,1,0:T(8,128)(2,1)S(1)}, u32[]{:S(2)}, u32[]{:S(2)}) %collective-permute-start.5) | collective-permute-done | bytes 131104 | tf_op jit(solution)/shard_map/ppermute | solution.py:373
  133.6 1.0 fusion.10
  134.7 4.4 %collective-permute-start.6 = (bf16[4,128,128]{2,1,0:T(8,128)(2,1)S(1)}, bf16[4,128,128]{2,1,0:T(8,128)(2,1)S(1)}, u32[]{:S(2)}, u32[]{:S(2)}) collective-permute-start(bf16[4,128,128]{2,1,0:T(8,128)(2,1)S(1)} %fusion.10), channel_id=1, source_target_pairs={{0,8},{8,16},{16,24},{1,9},{9,17},{17,25},{2,10},{10,18},{18,26},{... | collective-permute-start | bytes 393224 | tf_op jit(solution)/shard_map/ppermute | solution.py:373
  139.0 2.5 %collective-permute-done.6 = bf16[4,128,128]{2,1,0:T(8,128)(2,1)S(1)} collective-permute-done((bf16[4,128,128]{2,1,0:T(8,128)(2,1)S(1)}, bf16[4,128,128]{2,1,0:T(8,128)(2,1)S(1)}, u32[]{:S(2)}, u32[]{:S(2)}) %collective-permute-start.6) | collective-permute-done | bytes 131104 | tf_op jit(solution)/shard_map/ppermute | solution.py:373
  141.5 1.0 fusion.12
  142.6 4.4 %collective-permute-start.7 = (bf16[4,128,128]{2,1,0:T(8,128)(2,1)S(1)}, bf16[4,128,128]{2,1,0:T(8,128)(2,1)S(1)}, u32[]{:S(2)}, u32[]{:S(2)}) collective-permute-start(bf16[4,128,128]{2,1,0:T(8,128)(2,1)S(1)} %fusion.12), channel_id=1, source_target_pairs={{0,8},{8,16},{16,24},{1,9},{9,17},{17,25},{2,10},{10,18},{18,26},{... | collective-permute-start | bytes 393224 | tf_op jit(solution)/shard_map/ppermute | solution.py:373
  147.8 1.7 collective-permute-done.7.h0_ref
  150.1 41.7 %selective_scan.1 = bf16[128,8192]{1,0:T(8,128)(2,1)} custom-call(bf16[1024,1024]{1,0:T(8,128)(2,1)} %get-tuple-element.11.xc_ref, f32[8192,128]{1,0:T(8,128)} %get-tuple-element.13.st, f32[8192,128]{1,0:T(8,128)} %get-tuple-element.14.dr, f32[32768]{0:T(1024)} %reshape_reshape.4.bc_ref, f32[128,128]{1,0:T(8,128)} %reshape.21.rate_ref, ...), custom_call_target="tpu_custom_call" | custom-call | tf_op jit(solution)/shard_map/selective_scan/pallas_call | solution.py:329
  191.8 4.2 %fusion.4 = bf16[128,8192]{1,0:T(8,128)(2,1)} fusion(bf16[128,8192]{1,0:T(8,128)(2,1)S(1)} %copy-done.1, bf16[128,8192]{1,0:T(8,128)(2,1)} %selective_scan.1), kind=kLoop, calls=%fused_computation.6 | loop fusion | flops 8388608 | bytes 6291456 | tf_op jit(solution)/shard_map/convert_element_type | solution.py:407
  (38 shorter events, 6.1 us)
Async XLA Ops:
  0.0 8.5 %copy-start.8 = (bf16[1024]{0:T(1024)(128)(2,1)S(1)}, bf16[1024]{0:T(1024)(128)(2,1)}, u32[]{:S(2)}) copy-start(bf16[1024]{0:T(1024)(128)(2,1)} %param.13) | copy-start | bytes 6148
  0.0 8.5 %copy-start.5 = (bf16[4,1024]{1,0:T(4,128)(2,1)S(1)}, bf16[4,1024]{1,0:T(4,128)(2,1)}, u32[]{:S(2)}) copy-start(bf16[4,1024]{1,0:T(4,128)(2,1)} %param.12) | copy-start | bytes 24580
  0.0 9.2 %copy-start.4 = (f32[16,1024]{1,0:T(8,128)S(1)}, f32[16,1024]{1,0:T(8,128)}, u32[]{:S(2)}) copy-start(f32[16,1024]{1,0:T(8,128)} %param.18) | copy-start | bytes 196612
  0.0 9.2 %copy-start.6 = (f32[1024]{0:T(1024)S(1)}, f32[1024]{0:T(1024)}, u32[]{:S(2)}) copy-start(f32[1024]{0:T(1024)} %param.19) | copy-start | bytes 12292
  0.0 9.2 %copy-start.7 = (f32[1024]{0:T(1024)S(1)}, f32[1024]{0:T(1024)}, u32[]{:S(2)}) copy-start(f32[1024]{0:T(1024)} %param.17) | copy-start | bytes 12292
  0.0 9.9 %copy-start.9 = (bf16[256,1024]{1,0:T(8,128)(2,1)S(1)}, bf16[256,1024]{1,0:T(8,128)(2,1)}, u32[]{:S(2)}) copy-start(bf16[256,1024]{1,0:T(8,128)(2,1)} %param.16) | copy-start | bytes 1572868
  3.3 55.3 %all-to-all-start = ((bf16[128,8,1024]{2,0,1:T(8,128)(2,1)}), bf16[128,8,1024]{2,0,1:T(8,128)(2,1)S(1)}, u32[]{:S(2)}, u32[]{:S(2)}) async-start(bf16[128,8,1024]{2,0,1:T(8,128)(2,1)} %bitcast.32), calls=%async_computation | async-start | bytes 4194304 | tf_op jit(solution)/shard_map/all_to_all | solution.py:382
  8.5 4.6 %collective-permute-start.1 = (bf16[5,1024]{1,0:T(8,128)(2,1)S(1)}, bf16[5,1024]{1,0:T(8,128)(2,1)S(1)}, u32[]{:S(2)}, u32[]{:S(2)}) collective-permute-start(bf16[5,1024]{1,0:T(8,128)(2,1)S(1)} %pad_maximum_fusion.1), channel_id=1, source_target_pairs={{0,0},{2,8},{1,16},{3,24},{8,2},{10,10},{9,18},{11,26},{16,1},{18,... | collective-permute-start | bytes 30728 | tf_op jit(solution)/shard_map/ppermute | solution.py:371
  9.2 5.1 %collective-permute-start.4 = (f32[18,1024]{1,0:T(8,128)S(1)}, f32[18,1024]{1,0:T(8,128)S(1)}, u32[]{:S(2)}, u32[]{:S(2)}) collective-permute-start(f32[18,1024]{1,0:T(8,128)S(1)} %pad_maximum_fusion), channel_id=1, source_target_pairs={{0,0},{2,8},{1,16},{3,24},{8,2},{10,10},{9,18},{11,26},{16,1},{18,... | collective-permute-start | bytes 221192 | tf_op jit(solution)/shard_map/ppermute | solution.py:371
  9.9 94.4 %collective-permute-start.3 = (bf16[256,1024]{1,0:T(8,128)(2,1)S(1)}, bf16[256,1024]{1,0:T(8,128)(2,1)}, u32[]{:S(2)}, u32[]{:S(2)}) collective-permute-start(bf16[256,1024]{1,0:T(8,128)(2,1)S(1)} %copy-done.9), channel_id=1, source_target_pairs={{0,0},{2,8},{1,16},{3,24},{8,2},{10,10},{9,18},{11,26},{16,1},{18,... | collective-permute-start | bytes 1572872 | tf_op jit(solution)/shard_map/ppermute | solution.py:371
  11.4 54.2 %collective-permute-start.2 = (bf16[1024,288]{0,1:T(8,128)(2,1)}, bf16[1024,288]{0,1:T(8,128)(2,1)S(1)}, u32[]{:S(2)}, u32[]{:S(2)}) collective-permute-start(bf16[1024,288]{0,1:T(8,128)(2,1)} %param.14), channel_id=1, source_target_pairs={{0,0},{2,8},{1,16},{3,24},{8,2},{10,10},{9,18},{11,26},{16,1},{18,... | collective-permute-start | bytes 1769480 | tf_op jit(solution)/shard_map/ppermute | solution.py:371
  58.6 8.9 %copy-start = (bf16[128,8,1024]{2,0,1:T(8,128)(2,1)}, bf16[128,8,1024]{2,0,1:T(8,128)(2,1)S(1)}, u32[]{:S(2)}) copy-start(bf16[128,8,1024]{2,0,1:T(8,128)(2,1)S(1)} %all-to-all-done) | copy-start | bytes 6291460
  58.6 8.2 %collective-permute-start = (bf16[4,8,1024]{2,1,0:T(8,128)(2,1)S(1)}, bf16[4,8,1024]{2,1,0:T(8,128)(2,1)S(1)}, u32[]{:S(2)}, u32[]{:S(2)}) collective-permute-start(bf16[4,8,1024]{2,1,0:T(8,128)(2,1)S(1)} %slice.36), channel_id=1, source_target_pairs={{0,8},{8,16},{16,24},{1,9},{9,17},{17,25},{2,10},{10,18},{18,26},{... | collective-permute-start | bytes 196616 | tf_op jit(solution)/shard_map/ppermute | solution.py:373
  104.3 29.3 %copy-start.2 = (f32[128,128]{1,0:T(8,128)S(1)}, f32[128,128]{1,0:T(8,128)}, u32[]{:S(2)}) copy-start(f32[128,128]{1,0:T(8,128)} %reshape.21.rate_ref) | copy-start | bytes 196612
  127.3 6.3 %collective-permute-start.5 = (bf16[4,128,128]{2,1,0:T(8,128)(2,1)S(1)}, bf16[4,128,128]{2,1,0:T(8,128)(2,1)S(1)}, u32[]{:S(2)}, u32[]{:S(2)}) collective-permute-start(bf16[4,128,128]{2,1,0:T(8,128)(2,1)S(1)} %convert_element_type.45), channel_id=1, source_target_pairs={{0,8},{8,16},{16,24},{1,9},{9,17},{17,25},{2,10},{10,18},{18,26},{... | collective-permute-start | bytes 393224 | tf_op jit(solution)/shard_map/ppermute | solution.py:373
  134.7 6.9 %collective-permute-start.6 = (bf16[4,128,128]{2,1,0:T(8,128)(2,1)S(1)}, bf16[4,128,128]{2,1,0:T(8,128)(2,1)S(1)}, u32[]{:S(2)}, u32[]{:S(2)}) collective-permute-start(bf16[4,128,128]{2,1,0:T(8,128)(2,1)S(1)} %fusion.10), channel_id=1, source_target_pairs={{0,8},{8,16},{16,24},{1,9},{9,17},{17,25},{2,10},{10,18},{18,26},{... | collective-permute-start | bytes 393224 | tf_op jit(solution)/shard_map/ppermute | solution.py:373
  142.6 6.9 %collective-permute-start.7 = (bf16[4,128,128]{2,1,0:T(8,128)(2,1)S(1)}, bf16[4,128,128]{2,1,0:T(8,128)(2,1)S(1)}, u32[]{:S(2)}, u32[]{:S(2)}) collective-permute-start(bf16[4,128,128]{2,1,0:T(8,128)(2,1)S(1)} %fusion.12), channel_id=1, source_target_pairs={{0,8},{8,16},{16,24},{1,9},{9,17},{17,25},{2,10},{10,18},{18,26},{... | collective-permute-start | bytes 393224 | tf_op jit(solution)/shard_map/ppermute | solution.py:373
  149.4 0.7 copy-start.3
  150.1 41.7 %copy-start.1 = (bf16[128,8192]{1,0:T(8,128)(2,1)S(1)}, bf16[128,8192]{1,0:T(8,128)(2,1)}, u32[]{:S(2)}) copy-start(bf16[128,8192]{1,0:T(8,128)(2,1)} %param.11) | copy-start | bytes 6291460

commit v4 on v3

--- a/solution.py
+++ b/solution.py
@@ -104,6 +104,48 @@
         compiler_params=pltpu.CompilerParams(collective_id=0, has_side_effects=True),
         name="reduce_norm",
     )(partial, gain[None, :])
+
+
+def exchange_kernel(peers, in_ref, out_ref, send_sem, recv_sem):
+    rows = in_ref.shape[0]
+    chans = out_ref.shape[1]
+    me = greet(peers)
+    mine = pl.ds(pl.multiple_of(me * rows, rows), rows)
+    copies = []
+    for k in range(1, peers):
+        other = lax.rem(me + k, peers)
+        copy = pltpu.make_async_remote_copy(
+            src_ref=in_ref.at[:, pl.ds(pl.multiple_of(other * chans, chans), chans)],
+            dst_ref=out_ref.at[mine],
+            send_sem=send_sem.at[k],
+            recv_sem=recv_sem.at[k],
+            device_id=device(other),
+            device_id_type=MESH,
+        )
+        copy.start()
+        copies.append(copy)
+    out_ref[mine, :] = in_ref[:, pl.ds(pl.multiple_of(me * chans, chans), chans)]
+    for copy in copies:
+        copy.wait()
+
+
+def exchange(inputs, peers):
+    rows, total = inputs.shape
+    return pl.pallas_call(
+        functools.partial(exchange_kernel, peers),
+        in_specs=[pl.BlockSpec(memory_space=pltpu.VMEM)],
+        out_specs=pl.BlockSpec(memory_space=pltpu.VMEM),
+        out_shape=jax.ShapeDtypeStruct((peers * rows, total // peers), inputs.dtype),
+        scratch_shapes=[
+            pltpu.SemaphoreType.DMA((peers,)),
+            pltpu.SemaphoreType.DMA((peers,)),
+        ],
+        compiler_params=pltpu.CompilerParams(collective_id=2, has_side_effects=True),
+        cost_estimate=pl.CostEstimate(
+            flops=0, bytes_accessed=24 * rows * total, transcendentals=0
+        ),
+        name="exchange",
+    )(inputs)
 
 
 def conv_kernel(width, rank, x_ref, halo_ref, w_ref, b_ref, xw_ref, xc_ref, part_ref, prev):
@@ -379,7 +421,7 @@
     width = conv_weight.shape[0]
     conv_weight, conv_bias = conv_pack[:width], conv_pack[width]
 
-    arrived = lax.all_to_all(conv_input, PLANE, split_axis=1, concat_axis=0, tiled=True)
+    arrived = exchange(conv_input, conv_input.shape[1] // chans)
     span = arrived.shape[0] // parts
     halo = onward(arrived.reshape(parts, span, chans)[:, span - HALO :]).astype(jnp.float32)
     conv_out, partial_value = conv_project(

time: 197 us -> 210 us (1.066)
  Pallas kernels: 96.6 us -> 160 us
  waiting for transfers between devices: 50.9 us -> 7.35 us
  starting transfers between devices: 28 us -> 19.1 us
    pallas_call x0 -> x1, Pallas kernels: none -> 62.3 us  [exchange(): pl.pallas_call(functools.partial(exchange_kernel, peers), in_specs=[pl.Bl...]
    all_to_all x1 -> x0, waiting for transfers between devices: 44.2 us -> none  [local(): lax.all_to_all(conv_input, PLANE, split_axis=1, concat_axis=0, tiled=True)]
    all_to_all x1 -> x0, starting transfers between devices: 5.21 us -> none  [local(): lax.all_to_all(conv_input, PLANE, split_axis=1, concat_axis=0, tiled=True)]
    ppermute x4, starting transfers between devices: 18.3 us -> 14.4 us  [local(): onward = lambda v: lax.ppermute(v, 'z', following)]
    all_to_all x1 -> x0, local copies, waits for them, and re-layouts: 3.23 us -> none  [local(): lax.all_to_all(conv_input, PLANE, split_axis=1, concat_axis=0, tiled=True)]
  transfers between devices with their start and end apart: 9 -> 8, of which waited for: 4 -> 4; matrix products, arithmetic and copies ran while one was open for 5% -> 5% of each run, Pallas kernels for 17% -> 47%
where the time goes in v4:
time: 210 us; the launch traced here: 208 us
  Pallas kernels  160 us (76%)
  starting transfers between devices  19.1 us (9%)
  other arithmetic  11.9 us (6%)
  local copies, waits for them, and re-layouts  9.05 us (4%)
  waiting for transfers between devices  7.35 us (4%)
    pallas_call x1, Pallas kernels, exchange(): pl.pallas_call(functools.partial(exchange_kernel, peers), in_specs=[pl.Bl...  62.3 us
    pallas_call x1, Pallas kernels, scan(): pl.pallas_call(functools.partial(scan_kernel, states, parts, peers), in_s...  41.5 us
    pallas_call x1, Pallas kernels, reduce_norm(): pl.pallas_call(functools.partial(reduce_kernel, peers, rank, states2), in...  25.8 us
    pallas_call x1, Pallas kernels, prepare(): pl.pallas_call(functools.partial(prepare_kernel, states), grid=(parts, st...  21.9 us
    ppermute x4, starting transfers between devices, local(): onward = lambda v: lax.ppermute(v, 'z', following)  14.4 us
    pallas_call x1, Pallas kernels, conv_project(): pl.pallas_call(functools.partial(conv_kernel, width, rank), grid=(parts,...  8.61 us
    ppermute x4, waiting for transfers between devices, local(): onward = lambda v: lax.ppermute(v, 'z', following)  7.34 us
    ppermute x4, starting transfers between devices, local(): move = lambda v: lax.ppermute(v, ('z', 'x', 'core'), swap)  4.74 us
  transfers between devices with their start and end apart: 8, of which 4 were waited for; matrix products, arithmetic and copies ran while one was open for 5% of the time, Pallas kernels for 47%

profile of v4, /device:TPU:0, one launch (start us, length us, event | category | flops | bytes accessed | tf_op | source)
XLA Modules:
  0.0 207.7 jit_solution(5965645139829018548)
XLA Ops:
  2.1 0.9 pad_maximum_fusion
  3.6 1.7 collective-permute-start.3
  5.3 1.7 collective-permute-start.2
  7.0 62.3 %exchange.1.x_ref = bf16[1024,1024]{1,0:T(8,128)(2,1)} custom-call(bf16[128,8192]{1,0:T(8,128)(2,1)} %in_ref.1), custom_call_target="tpu_custom_call" | custom-call | bytes 25165824 | tf_op jit(solution)/shard_map/exchange/pallas_call | solution.py:134
  69.3 0.8 slice.36
  70.2 1.3 collective-permute-start
  75.3 1.2 copy.14.xw_ref
  76.4 8.6 %conv_project.1 = (bf16[1024,1024]{1,0:T(8,128)(2,1)}, bf16[1024,384]{1,0:T(8,128)(2,1)}) custom-call(bf16[1024,1024]{1,0:T(8,128)(2,1)} %exchange.1.x_ref, f32[4,8,1024]{2,1,0:T(8,128)} %convert_element_type.40.halo_ref, f32[4,1024]{1,0:T(4,128)} %slice_convert_fusion.w_ref, f32[1,1024]{1,0:T(1,128)} %slice_convert_fusion.1.b_ref, ...), custom_call_target="tpu_custom_call" | custom-call | tf_op jit(solution)/shard_map/conv_project/pallas_call | solution.py:180
  85.1 25.8 %reduce_norm.1 = bf16[1024,384]{1,0:T(8,128)(2,1)} custom-call(bf16[1024,384]{1,0:T(8,128)(2,1)} %get-tuple-element.12.part_ref, f32[1,256]{1,0:T(1,128)} %bitcast.25), custom_call_target="tpu_custom_call" | custom-call | tf_op jit(solution)/shard_map/reduce_norm/pallas_call | solution.py:94
  110.9 1.9 slice.30.nm_ref
  112.8 1.2 convert_add_fusion
  114.0 0.9 reshape.18.bc_ref
  115.8 21.9 %prepare.1 = (f32[8192,128]{1,0:T(8,128)}, f32[8192,128]{1,0:T(8,128)}, f32[4,128,128]{2,1,0:T(8,128)}, f32[4,8,128]{2,1,0:T(8,128)}) custom-call(bf16[1024,1024]{1,0:T(8,128)(2,1)} %get-tuple-element.11.xc_ref, bf16[1024,256]{1,0:T(8,128)(2,1)} %slice.30.nm_ref, f32[8,1,4096]{2,1,0:T(1,128)} %reshape.18.bc_ref, bf16[256,1024]{1,0:T(8,128)(2,1)} %copy-done.3, ...), custom_call_target="tpu_custom_call" | custom-call | flops 620756992 | bytes 10485760 | tf_op jit(solution)/shard_map/prepare/pallas_call | solution.py:250
  137.7 1.0 convert_element_type.45
  138.7 4.4 %collective-permute-start.5 = (bf16[4,128,128]{2,1,0:T(8,128)(2,1)S(1)}, bf16[4,128,128]{2,1,0:T(8,128)(2,1)S(1)}, u32[]{:S(2)}, u32[]{:S(2)}) collective-permute-start(bf16[4,128,128]{2,1,0:T(8,128)(2,1)S(1)} %convert_element_type.45), channel_id=1, source_target_pairs={{0,8},{8,16},{16,24},{1,9},{9,17},{17,25},{2,10},{10,18},{18,26},{... | collective-permute-start | bytes 393224 | tf_op jit(solution)/shard_map/ppermute | solution.py:415
  143.1 2.5 %collective-permute-done.5 = bf16[4,128,128]{2,1,0:T(8,128)(2,1)S(1)} collective-permute-done((bf16[4,128,128]{2,1,0:T(8,128)(2,1)S(1)}, bf16[4,128,128]{2,1,0:T(8,128)(2,1)S(1)}, u32[]{:S(2)}, u32[]{:S(2)}) %collective-permute-start.5) | collective-permute-done | bytes 131104 | tf_op jit(solution)/shard_map/ppermute | solution.py:415
  145.6 1.0 fusion.10
  146.6 4.4 %collective-permute-start.6 = (bf16[4,128,128]{2,1,0:T(8,128)(2,1)S(1)}, bf16[4,128,128]{2,1,0:T(8,128)(2,1)S(1)}, u32[]{:S(2)}, u32[]{:S(2)}) collective-permute-start(bf16[4,128,128]{2,1,0:T(8,128)(2,1)S(1)} %fusion.10), channel_id=1, source_target_pairs={{0,8},{8,16},{16,24},{1,9},{9,17},{17,25},{2,10},{10,18},{18,26},{... | collective-permute-start | bytes 393224 | tf_op jit(solution)/shard_map/ppermute | solution.py:415
  151.0 2.5 %collective-permute-done.6 = bf16[4,128,128]{2,1,0:T(8,128)(2,1)S(1)} collective-permute-done((bf16[4,128,128]{2,1,0:T(8,128)(2,1)S(1)}, bf16[4,128,128]{2,1,0:T(8,128)(2,1)S(1)}, u32[]{:S(2)}, u32[]{:S(2)}) %collective-permute-start.6) | collective-permute-done | bytes 131104 | tf_op jit(solution)/shard_map/ppermute | solution.py:415
  153.5 1.0 fusion.12
  154.5 4.4 %collective-permute-start.7 = (bf16[4,128,128]{2,1,0:T(8,128)(2,1)S(1)}, bf16[4,128,128]{2,1,0:T(8,128)(2,1)S(1)}, u32[]{:S(2)}, u32[]{:S(2)}) collective-permute-start(bf16[4,128,128]{2,1,0:T(8,128)(2,1)S(1)} %fusion.12), channel_id=1, source_target_pairs={{0,8},{8,16},{16,24},{1,9},{9,17},{17,25},{2,10},{10,18},{18,26},{... | collective-permute-start | bytes 393224 | tf_op jit(solution)/shard_map/ppermute | solution.py:415
  159.7 1.7 collective-permute-done.7.h0_ref
  162.0 41.5 %selective_scan.1 = bf16[128,8192]{1,0:T(8,128)(2,1)} custom-call(bf16[1024,1024]{1,0:T(8,128)(2,1)} %get-tuple-element.11.xc_ref, f32[8192,128]{1,0:T(8,128)} %get-tuple-element.13.st, f32[8192,128]{1,0:T(8,128)} %get-tuple-element.14.dr, f32[32768]{0:T(1024)} %reshape_reshape.4.bc_ref, f32[128,128]{1,0:T(8,128)} %reshape.17.rate_ref, ...), custom_call_target="tpu_custom_call" | custom-call | tf_op jit(solution)/shard_map/selective_scan/pallas_call | solution.py:371
  203.6 4.2 %fusion.4 = bf16[128,8192]{1,0:T(8,128)(2,1)} fusion(bf16[128,8192]{1,0:T(8,128)(2,1)S(1)} %copy-done, bf16[128,8192]{1,0:T(8,128)(2,1)} %selective_scan.1), kind=kLoop, calls=%fused_computation.6 | loop fusion | flops 8388608 | bytes 6291456 | tf_op jit(solution)/shard_map/convert_element_type | solution.py:449
  (24 shorter events, 8.8 us)
Async XLA Ops:
  1.4 70.1 %collective-permute-start.1 = (bf16[5,1024]{1,0:T(8,128)(2,1)S(1)}, bf16[5,1024]{1,0:T(8,128)(2,1)S(1)}, u32[]{:S(2)}, u32[]{:S(2)}) collective-permute-start(bf16[5,1024]{1,0:T(8,128)(2,1)S(1)} %pad_maximum_fusion.1), channel_id=1, source_target_pairs={{0,0},{2,8},{1,16},{3,24},{8,2},{10,10},{9,18},{11,26},{16,1},{18,... | collective-permute-start | bytes 30728 | tf_op jit(solution)/shard_map/ppermute | solution.py:413
  3.0 71.1 %collective-permute-start.4 = (f32[18,1024]{1,0:T(8,128)S(1)}, f32[18,1024]{1,0:T(8,128)S(1)}, u32[]{:S(2)}, u32[]{:S(2)}) collective-permute-start(f32[18,1024]{1,0:T(8,128)S(1)} %pad_maximum_fusion), channel_id=1, source_target_pairs={{0,0},{2,8},{1,16},{3,24},{8,2},{10,10},{9,18},{11,26},{16,1},{18,... | collective-permute-start | bytes 221192 | tf_op jit(solution)/shard_map/ppermute | solution.py:413
  3.6 111.3 %collective-permute-start.3 = (bf16[256,1024]{1,0:T(8,128)(2,1)}, bf16[256,1024]{1,0:T(8,128)(2,1)S(1)}, u32[]{:S(2)}, u32[]{:S(2)}) collective-permute-start(bf16[256,1024]{1,0:T(8,128)(2,1)} %param.16), channel_id=1, source_target_pairs={{0,0},{2,8},{1,16},{3,24},{8,2},{10,10},{9,18},{11,26},{16,1},{18,... | collective-permute-start | bytes 1572872 | tf_op jit(solution)/shard_map/ppermute | solution.py:413
  5.3 70.0 %collective-permute-start.2 = (bf16[1024,288]{0,1:T(8,128)(2,1)}, bf16[1024,288]{0,1:T(8,128)(2,1)S(1)}, u32[]{:S(2)}, u32[]{:S(2)}) collective-permute-start(bf16[1024,288]{0,1:T(8,128)(2,1)} %param.14), channel_id=1, source_target_pairs={{0,0},{2,8},{1,16},{3,24},{8,2},{10,10},{9,18},{11,26},{16,1},{18,... | collective-permute-start | bytes 1769480 | tf_op jit(solution)/shard_map/ppermute | solution.py:413
  70.2 3.2 %collective-permute-start = (bf16[4,8,1024]{2,1,0:T(8,128)(2,1)S(1)}, bf16[4,8,1024]{2,1,0:T(8,128)(2,1)S(1)}, u32[]{:S(2)}, u32[]{:S(2)}) collective-permute-start(bf16[4,8,1024]{2,1,0:T(8,128)(2,1)S(1)} %slice.36), channel_id=1, source_target_pairs={{0,8},{8,16},{16,24},{1,9},{9,17},{17,25},{2,10},{10,18},{18,26},{... | collective-permute-start | bytes 196616 | tf_op jit(solution)/shard_map/ppermute | solution.py:415
  114.9 0.8 copy-start.3
  115.8 29.8 %copy-start.1 = (f32[128,128]{1,0:T(8,128)S(1)}, f32[128,128]{1,0:T(8,128)}, u32[]{:S(2)}) copy-start(f32[128,128]{1,0:T(8,128)} %reshape.17.rate_ref) | copy-start | bytes 196612
  138.7 6.9 %collective-permute-start.5 = (bf16[4,128,128]{2,1,0:T(8,128)(2,1)S(1)}, bf16[4,128,128]{2,1,0:T(8,128)(2,1)S(1)}, u32[]{:S(2)}, u32[]{:S(2)}) collective-permute-start(bf16[4,128,128]{2,1,0:T(8,128)(2,1)S(1)} %convert_element_type.45), channel_id=1, source_target_pairs={{0,8},{8,16},{16,24},{1,9},{9,17},{17,25},{2,10},{10,18},{18,26},{... | collective-permute-start | bytes 393224 | tf_op jit(solution)/shard_map/ppermute | solution.py:415
  146.6 6.9 %collective-permute-start.6 = (bf16[4,128,128]{2,1,0:T(8,128)(2,1)S(1)}, bf16[4,128,128]{2,1,0:T(8,128)(2,1)S(1)}, u32[]{:S(2)}, u32[]{:S(2)}) collective-permute-start(bf16[4,128,128]{2,1,0:T(8,128)(2,1)S(1)} %fusion.10), channel_id=1, source_target_pairs={{0,8},{8,16},{16,24},{1,9},{9,17},{17,25},{2,10},{10,18},{18,26},{... | collective-permute-start | bytes 393224 | tf_op jit(solution)/shard_map/ppermute | solution.py:415
  154.5 6.9 %collective-permute-start.7 = (bf16[4,128,128]{2,1,0:T(8,128)(2,1)S(1)}, bf16[4,128,128]{2,1,0:T(8,128)(2,1)S(1)}, u32[]{:S(2)}, u32[]{:S(2)}) collective-permute-start(bf16[4,128,128]{2,1,0:T(8,128)(2,1)S(1)} %fusion.12), channel_id=1, source_target_pairs={{0,8},{8,16},{16,24},{1,9},{9,17},{17,25},{2,10},{10,18},{18,26},{... | collective-permute-start | bytes 393224 | tf_op jit(solution)/shard_map/ppermute | solution.py:415
  161.4 0.7 copy-start.2
  162.0 41.5 %copy-start = (bf16[128,8192]{1,0:T(8,128)(2,1)S(1)}, bf16[128,8192]{1,0:T(8,128)(2,1)}, u32[]{:S(2)}) copy-start(bf16[128,8192]{1,0:T(8,128)(2,1)} %param.11) | copy-start | bytes 6291460
